TPU v7x, 32 devices: a whole 2x2x4 slice. The times are simulated.
32 devices in a mesh: groups: 2 (over x), ctx: 16 (over z, y, core), tp: 1.
Axes of the slice: x: 2, y: 2, z: 4, core: 2. Of those that a mesh axis runs over, the one named last changes fastest.
Arguments:
- query_states: bfloat16 [8192, 32, 128], P(('groups', 'ctx'), 'tp'), parts along dimension 0, may hold values from -8 to 8
- key_states: bfloat16 [8192, 4, 128], P(('groups', 'ctx'), 'tp'), parts along dimension 0, may hold values from -8 to 8
- value_rows: bfloat16 [8192, 4, 128], P(('groups', 'ctx'), 'tp'), parts along dimension 0, may hold values from -12 to 12
- positions: int32 [8192], P(('groups', 'ctx')), parts along dimension 0, may hold values from 0 to 4095, as said below
- out_weight: bfloat16 [4096, 4096], P('tp', 'ctx'), may hold values from -0.375 to 0.375
Outputs:
- projected: bfloat16 [8192, 4096], P(('groups', 'ctx'), 'tp'), parts along dimension 0
There are 2 independent parts, one for each index of `groups`. A program takes and returns all parts, laid end to end along the dimension named above; an argument that names none is the same for every part. Nothing has to cross between parts.
Inputs may be any that keep to these rules, and one draw needn't show every extreme that they name: Each of 0 to 4095 appears once. Half-block b holds positions b * 128 to (b + 1) * 128 - 1. The 256 rows of one device along ctx hold half-block j and then half-block 32 - 1 - j, each in rising order, for a j below 16 that differs from device to device.
All inputs are finite; a program needn't handle non-finite values.
Results may differ from a plain program's by a relative error of at most 0.01.
Values may be sent and summed in bfloat16 or wider, within the bound.
A program may use at most 128 MiB of HBM per device.

v0:
```python
import functools
import math

import jax
import jax.numpy as jnp
from jax import lax
from jax.experimental import pallas as pl
from jax.experimental.pallas import tpu as pltpu
from jax.sharding import PartitionSpec as P

LOW_START = -1e30
BLOCKS_PER_STEP = 4
CHUNK = 1024
TAIL = 16


def attend_kernel(half, group, place_ref, own_ref, q_ref, k_ref, v_ref, out_ref, acc_ref, max_ref, sum_ref):
    rows = group * half
    head_size = q_ref.shape[-1]
    span = BLOCKS_PER_STEP * half
    chunk = min(CHUNK, rows)
    to_exp2 = head_size ** (-0.5) * math.log2(math.e)

    def step(which, number, masked, query_block):
        keys, values = [], []
        for i in range(BLOCKS_PER_STEP):
            place = place_ref[number * BLOCKS_PER_STEP + i]
            keys.append(k_ref[pl.ds(pl.multiple_of(place, TAIL), half), :])
            values.append(v_ref[pl.ds(pl.multiple_of(place, TAIL), half), :])
        key_part = jnp.concatenate(keys, axis=0)
        value_part = jnp.concatenate(values, axis=0)
        if masked:
            key_place = number * span + lax.broadcasted_iota(jnp.int32, (span, chunk), 0)
            query_place = query_block * half + lax.broadcasted_iota(jnp.int32, (span, chunk), 1) % half
            visible = key_place <= query_place
        for c in range(rows // chunk):
            cols = pl.ds(c * chunk, chunk)
            scores = lax.dot_general(
                key_part,
                q_ref[0, which, cols, :],
                (((1,), (1,)), ((), ())),
                preferred_element_type=jnp.float32,
            )
            if masked:
                scores = jnp.where(visible, scores, LOW_START)
            old_max = max_ref[:, cols]
            new_max = jnp.maximum(old_max, jnp.max(scores, axis=0, keepdims=True))
            factor = jnp.exp2((old_max - new_max) * to_exp2)
            exp_scores = jnp.exp2((scores - new_max) * to_exp2)
            max_ref[:, cols] = new_max
            sum_ref[:, cols] = sum_ref[:, cols] * factor + jnp.sum(exp_scores, axis=0, keepdims=True)
            weighted = lax.dot_general(
                value_part,
                exp_scores.astype(jnp.bfloat16),
                (((0,), (0,)), ((), ())),
                preferred_element_type=jnp.float32,
            )
            acc_ref[:, cols] = acc_ref[:, cols] * factor + weighted

    for which in range(2):
        query_block = own_ref[which]
        steps = query_block // BLOCKS_PER_STEP
        max_ref[...] = jnp.full_like(max_ref, LOW_START)
        sum_ref[...] = jnp.zeros_like(sum_ref)
        acc_ref[...] = jnp.zeros_like(acc_ref)

        @pl.loop(0, steps)
        def _(number):
            step(which, number, False, query_block)

        step(which, steps, True, query_block)
        for g in range(group):
            cols = pl.ds(g * half, half)
            attended = acc_ref[:, cols] / sum_ref[:, cols]
            out_ref[pl.ds(g * head_size, head_size), pl.ds(which * half, half)] = attended.astype(jnp.bfloat16)


def attend(query_parts, gathered, place, own, first_head, all_heads, half):
    kv_heads, _, rows, head_size = query_parts.shape
    keys_total = gathered.shape[0]
    blocks = place.shape[0]
    group = rows // half
    flops = 4 * kv_heads * rows * head_size * half * (blocks + 1)
    return pl.pallas_call(
        functools.partial(attend_kernel, half, group),
        out_shape=jax.ShapeDtypeStruct((kv_heads * group * head_size, 2 * half), jnp.bfloat16),
        grid_spec=pltpu.PrefetchScalarGridSpec(
            num_scalar_prefetch=2,
            grid=(kv_heads,),
            in_specs=[
                pl.BlockSpec((1, 2, rows, head_size), lambda h, *_: (h, 0, 0, 0)),
                pl.BlockSpec((keys_total, head_size), lambda h, *_: (0, h + first_head)),
                pl.BlockSpec((keys_total, head_size), lambda h, *_: (0, h + first_head + all_heads)),
            ],
            out_specs=pl.BlockSpec((group * head_size, 2 * half), lambda h, *_: (h, 0)),
            scratch_shapes=[
                pltpu.VMEM((head_size, rows), jnp.float32),
                pltpu.VMEM((1, rows), jnp.float32),
                pltpu.VMEM((1, rows), jnp.float32),
            ],
        ),
        compiler_params=pltpu.CompilerParams(
            dimension_semantics=("arbitrary",), vmem_limit_bytes=20 * 1024 * 1024
        ),
        cost_estimate=pl.CostEstimate(
            flops=flops, bytes_accessed=2 * gathered.size, transcendentals=flops // (4 * head_size)
        ),
        name="attend",
    )(place, own, query_parts, gathered, gathered)


def spread_kernel(devices, own_ref, out_ref, far_send, far_recv, side_send, side_recv, pair_send, pair_recv, own_sem):
    me = lax.axis_index("ctx")
    outers = devices // 4
    outer, middle, inner = me // 4, (me // 2) % 2, me % 2

    def at(o, m, i):
        return (o * 2 + m) * 2 + i

    side = at(outer, 1 - middle, inner)
    pair = at(outer, middle, 1 - inner)
    far = [at((outer + k) % outers, middle, inner) for k in range(1, outers)]
    barrier = pltpu.get_barrier_semaphore()
    for other in far + [side, pair]:
        pl.semaphore_signal(barrier, inc=1, device_id={"ctx": other}, device_id_type=pl.DeviceIdType.MESH)
    pl.semaphore_wait(barrier, outers + 1)

    def send(source, slot, sends, recvs, number, target):
        return pltpu.make_async_remote_copy(
            src_ref=source,
            dst_ref=out_ref.at[slot],
            send_sem=sends.at[number],
            recv_sem=recvs.at[number],
            device_id={"ctx": target},
            device_id_type=pl.DeviceIdType.MESH,
        )

    own = pltpu.make_async_copy(own_ref, out_ref.at[me], own_sem)
    far_copies = [send(own_ref, me, far_send, far_recv, k, far[k]) for k in range(outers - 1)]
    for copy in far_copies:
        copy.start()
    side_copies = [send(own_ref, me, side_send, side_recv, 0, side)]
    pair_copies = [send(own_ref, me, pair_send, pair_recv, 0, pair)]
    side_copies[0].start()
    pair_copies[0].start()
    own.start()
    for k in range(outers - 1):
        far_copies[k].wait_recv()
        slot = at((outer + outers - 1 - k) % outers, middle, inner)
        side_copies.append(send(out_ref.at[slot], slot, side_send, side_recv, k + 1, side))
        pair_copies.append(send(out_ref.at[slot], slot, pair_send, pair_recv, k + 1, pair))
        side_copies[-1].start()
        pair_copies[-1].start()
    for k in range(outers):
        side_copies[k].wait_recv()
        slot = at((outer + outers - k) % outers, 1 - middle, inner)
        pair_copies.append(send(out_ref.at[slot], slot, pair_send, pair_recv, outers + k, pair))
        pair_copies[-1].start()
    for copy in pair_copies:
        copy.wait_recv()
    for copy in far_copies + side_copies + pair_copies:
        copy.wait_send()
    own.wait()


def spread(packed):
    devices = lax.axis_size("ctx")
    outers = devices // 4
    rows, columns = packed.shape
    gathered = pl.pallas_call(
        functools.partial(spread_kernel, devices),
        out_shape=jax.ShapeDtypeStruct((devices, rows, columns), packed.dtype),
        in_specs=[pl.BlockSpec(memory_space=pltpu.VMEM)],
        out_specs=pl.BlockSpec(memory_space=pltpu.VMEM),
        scratch_shapes=[
            pltpu.SemaphoreType.DMA((outers - 1,)),
            pltpu.SemaphoreType.DMA((outers - 1,)),
            pltpu.SemaphoreType.DMA((outers,)),
            pltpu.SemaphoreType.DMA((outers,)),
            pltpu.SemaphoreType.DMA((2 * outers,)),
            pltpu.SemaphoreType.DMA((2 * outers,)),
            pltpu.SemaphoreType.DMA,
        ],
        compiler_params=pltpu.CompilerParams(
            collective_id=0, has_side_effects=True, vmem_limit_bytes=24 * 1024 * 1024
        ),
        cost_estimate=pl.CostEstimate(flops=0, bytes_accessed=20 * packed.size * devices, transcendentals=0),
        name="spread",
    )(packed)
    return gathered


def hand_on(value, by):
    parts = lax.axis_size("groups")
    return lax.ppermute(value, "groups", [(i, (i + by) % parts) for i in range(parts)])


def weave_kernel(share, me_ref, *refs):
    *shares, out_ref = refs
    parts = len(shares)
    for p in range(parts):
        by = lax.rem(p - me_ref[0] + parts, parts)
        chosen = shares[0][...]
        for k in range(1, parts):
            chosen = jnp.where(by == k, shares[k][...], chosen)
        for i in range(chosen.shape[1] // share):
            out_ref[:, (i * parts + p) * share : (i * parts + p + 1) * share] = chosen[:, i * share : (i + 1) * share]


def weave(results, me_part, devices):
    parts = len(results)
    tokens, columns = results[0].shape
    share = columns // devices
    return pl.pallas_call(
        functools.partial(weave_kernel, share),
        out_shape=jax.ShapeDtypeStruct((tokens, parts * columns), results[0].dtype),
        grid_spec=pltpu.PrefetchScalarGridSpec(
            num_scalar_prefetch=1,
            grid=(devices // 4,),
            in_specs=[pl.BlockSpec((tokens, 4 * share), lambda i, *_: (0, i))] * parts,
            out_specs=pl.BlockSpec((tokens, 4 * parts * share), lambda i, *_: (0, i)),
        ),
        name="weave",
    )(me_part.astype(jnp.int32).reshape(1), *results)


def local(query_states, key_states, value_rows, positions, out_weight):
    tokens, query_heads, head_size = query_states.shape
    kv_heads = key_states.shape[1]
    group = query_heads // kv_heads
    half = tokens // 2
    devices = lax.axis_size("ctx")
    blocks = 2 * devices
    parts = lax.axis_size("groups")
    me_part = lax.axis_index("groups")
    share = out_weight.shape[1] // parts
    weight_share = lax.dynamic_slice_in_dim(out_weight, me_part * share, share, 1)
    weight = lax.all_gather(weight_share, "ctx", axis=1, tiled=True)
    packed = jnp.concatenate(
        [key_states.reshape(tokens, kv_heads * head_size), value_rows.reshape(tokens, kv_heads * head_size)], axis=1
    )
    first = positions[0] // half
    tail = jnp.broadcast_to(first.astype(packed.dtype), (TAIL, packed.shape[1]))
    gathered = spread(jnp.concatenate([packed, tail], axis=0))
    firsts = gathered[:, tokens, 0].astype(jnp.int32)
    gathered = gathered.reshape(devices * (tokens + TAIL), packed.shape[1])
    wanted = jnp.arange(blocks, dtype=jnp.int32)[:, None]
    stored = jnp.stack([firsts, blocks - 1 - firsts], axis=1).reshape(1, blocks)
    kept = jnp.arange(blocks, dtype=jnp.int32)[None, :]
    starts = kept // 2 * (tokens + TAIL) + kept % 2 * half
    place = jnp.sum(jnp.where(stored == wanted, starts, 0), axis=1)
    place = place.astype(jnp.int32)
    own = jnp.stack([first, blocks - 1 - first]).astype(jnp.int32)
    query_parts = query_states.reshape(2, half, kv_heads, group, head_size).transpose(2, 0, 3, 1, 4)
    query_parts = query_parts.reshape(kv_heads, 2, group * half, head_size)
    pieces = min(2, kv_heads)
    span = kv_heads // pieces
    attended = [
        attend(query_parts[i * span : (i + 1) * span], gathered, place, own, i * span, kv_heads, half) for i in range(pieces)
    ]

    def project(rows):
        product = lax.dot_general(
            jnp.concatenate(rows, axis=0), weight, (((0,), (0,)), ((), ())), preferred_element_type=jnp.float32
        )
        return product.astype(jnp.bfloat16)

    guests = [[hand_on(piece, by) for piece in attended] for by in range(1, parts)]
    mine = project(attended)
    results = [mine] + [hand_on(project(rows), parts - 1 - i) for i, rows in enumerate(guests)]
    if share % 128 == 0:
        combined = weave(results, me_part, devices)
    else:
        shares = jnp.stack([r.reshape(tokens, devices, share) for r in results])
        order = (jnp.arange(parts) - me_part) % parts
        combined = jnp.moveaxis(jnp.take(shares, order, axis=0), 0, 2).reshape(tokens, devices * parts * share)
    return lax.psum_scatter(combined, "tp", scatter_dimension=1, tiled=True)


def solution(mesh):
    in_specs = (
        P(("groups", "ctx"), "tp", None),
        P(("groups", "ctx"), "tp", None),
        P(("groups", "ctx"), "tp", None),
        P(("groups", "ctx")),
        P("tp", "ctx"),
    )
    out_specs = P(("groups", "ctx"), "tp")
    return jax.shard_map(local, mesh=mesh, in_specs=in_specs, out_specs=out_specs, check_vma=False)
```

profile of v0, /device:TPU:24, one launch (start us, length us, event | category | flops | bytes accessed | tf_op | source)
XLA Modules:
  0.0 271.0 jit_solution(68544719613618603)
XLA Ops:
  6.6 1.5 copy-done
  8.1 1.0 constant_dynamic-slice_fusion
  9.2 0.6 slice.18
  12.5 129.6 %spread.1 = bf16[16,272,1024]{2,1,0:T(8,128)(2,1)S(1)} custom-call(bf16[272,1024]{1,0:T(8,128)(2,1)S(1)} %fusion.8.own_ref), custom_call_target="tpu_custom_call" | custom-call | bytes 89128960 | tf_op jit(solution)/shard_map/spread/pallas_call | solution.py:170
  142.0 0.4 convert_reduce_fusion
  142.4 3.4 %copy-done.1 = bf16[16,272,1024]{2,1,0:T(8,128)(2,1)} copy-done((bf16[16,272,1024]{2,1,0:T(8,128)(2,1)}, bf16[16,272,1024]{2,1,0:T(8,128)(2,1)S(1)}, u32[]{:S(2)}) %copy-start.1) | copy-done | bytes 8912920
  145.9 0.1 copy.10
  146.0 0.1 eq.17
  146.1 2.4 copy.17
  148.6 0.1 select_reduce_fusion.place_ref
  148.7 0.2 fusion.14
  148.9 3.5 %copy-done.2 = bf16[16,272,1024]{2,1,0:T(8,128)(2,1)S(1)} copy-done((bf16[16,272,1024]{2,1,0:T(8,128)(2,1)S(1)}, bf16[16,272,1024]{2,1,0:T(8,128)(2,1)}, u32[]{:S(2)}) %copy-start.2) | copy-done | bytes 8912920
  152.5 22.5 %attend.2 = bf16[2048,256]{1,0:T(8,128)(2,1)S(1)} custom-call(s32[32]{0:T(128)S(1)} %select_reduce_fusion.place_ref, s32[2]{0:T(128)S(1)} %pad_add_fusion.1.own_ref, bf16[2,2,1024,128]{3,2,1,0:T(8,128)(2,1)S(1)} %bitcast.26, bf16[4352,1024]{1,0:T(8,128)(2,1)S(1)} %bitcast.21, bf16[4352,1024]{1,0:T(8,128)(2,1)S(1)} %bitcast.22), custom_call_target="tpu_custom_call" | custom-call | flops 4429185024 | bytes 8912896 | tf_op jit(solution)/shard_map/attend/pallas_call | solution.py:84
  175.0 1.6 collective-permute-start
  176.5 22.7 %attend.3 = bf16[2048,256]{1,0:T(8,128)(2,1)S(1)} custom-call(s32[32]{0:T(128)S(1)} %select_reduce_fusion.place_ref, s32[2]{0:T(128)S(1)} %pad_add_fusion.1.own_ref, bf16[2,2,1024,128]{3,2,1,0:T(8,128)(2,1)S(1)} %bitcast.25, bf16[4352,1024]{1,0:T(8,128)(2,1)S(1)} %bitcast.23, bf16[4352,1024]{1,0:T(8,128)(2,1)S(1)} %bitcast.24), custom_call_target="tpu_custom_call" | custom-call | flops 4429185024 | bytes 8912896 | tf_op jit(solution)/shard_map/attend/pallas_call | solution.py:84
  199.3 0.6 collective-permute-start.1
  199.9 0.7 collective-permute-done
  200.5 1.0 copy-done.8
  201.5 23.2 %collective-permute-done.1 = bf16[2048,256]{1,0:T(8,128)(2,1)} collective-permute-done((bf16[2048,256]{1,0:T(8,128)(2,1)S(1)}, bf16[2048,256]{1,0:T(8,128)(2,1)}, u32[]{:S(2)}, u32[]{:S(2)}) %collective-permute-start.1) | collective-permute-done | bytes 1048608 | tf_op jit(solution)/shard_map/ppermute | solution.py:195
  224.7 11.0 %convolution_convert_fusion = bf16[256,2048]{1,0:T(8,128)(2,1)S(1)} fusion(bf16[4096,2048]{1,0:T(8,128)(2,1)} %all-gather.2.cloned.1.call-done, bf16[2048,256]{1,0:T(8,128)(2,1)} %collective-permute-done.1, bf16[2048,256]{1,0:T(8,128)(2,1)} %copy-done.8), kind=kOutput, calls=%fused_computation | convolution fusion | flops 4299685888 | bytes 19922944 | tf_op jit(solution)/shard_map/dot_general | solution.py:263
  235.7 0.6 collective-permute-start.2
  236.3 5.5 %convolution_convert_fusion.1.refs_0_ = bf16[256,2048]{1,0:T(8,128)(2,1)} fusion(bf16[4096,2048]{1,0:T(8,128)(2,1)S(1)} %copy-done.7, bf16[2048,256]{1,0:T(8,128)(2,1)S(1)} %copy-done.4, bf16[2048,256]{1,0:T(8,128)(2,1)S(1)} %attend.2), kind=kOutput, calls=%fused_computation.1 | convolution fusion | flops 4299685888 | bytes 19922944 | tf_op jit(solution)/shard_map/dot_general | solution.py:263
  241.8 18.5 %collective-permute-done.2.refs_1_ = bf16[256,2048]{1,0:T(8,128)(2,1)} collective-permute-done((bf16[256,2048]{1,0:T(8,128)(2,1)S(1)}, bf16[256,2048]{1,0:T(8,128)(2,1)}, u32[]{:S(2)}, u32[]{:S(2)}) %collective-permute-start.2) | collective-permute-done | bytes 1048608 | tf_op jit(solution)/shard_map/ppermute | solution.py:195
  260.3 3.9 %weave.1 = bf16[256,4096]{1,0:T(8,128)(2,1)} custom-call(s32[1]{0:T(128)} %bitcast.me_ref, bf16[256,2048]{1,0:T(8,128)(2,1)} %convolution_convert_fusion.1.refs_0_, bf16[256,2048]{1,0:T(8,128)(2,1)} %collective-permute-done.2.refs_1_), custom_call_target="tpu_custom_call" | custom-call | tf_op jit(solution)/shard_map/weave/pallas_call | solution.py:214
  (25 shorter events, 0.3 us)
Async XLA Ops:
  6.5 1.6 copy-start
  6.5 2.7 copy-start.9
  6.5 5.8 %copy-start.6 = (bf16[256,4,128]{2,1,0:T(4,128)(2,1)S(1)}, bf16[256,4,128]{2,1,0:T(4,128)(2,1)}, u32[]{:S(2)}) copy-start(bf16[256,4,128]{2,1,0:T(4,128)(2,1)} %param.6) | copy-start | bytes 786436
  6.5 5.8 %copy-start.5 = (bf16[256,4,128]{2,1,0:T(4,128)(2,1)S(1)}, bf16[256,4,128]{2,1,0:T(4,128)(2,1)}, u32[]{:S(2)}) copy-start(bf16[256,4,128]{2,1,0:T(4,128)(2,1)} %param.7) | copy-start | bytes 786436
  6.5 218.1 %all-gather.2.cloned.1.call-start = ((), (), s32[]{:S(2)}) async-start(), calls=%async_computation | async-start | bytes 17825792 | tf_op jit(solution)/shard_map/all_gather | solution.py:238
  142.4 3.4 %copy-start.1 = (bf16[16,272,1024]{2,1,0:T(8,128)(2,1)}, bf16[16,272,1024]{2,1,0:T(8,128)(2,1)S(1)}, u32[]{:S(2)}) copy-start(bf16[16,272,1024]{2,1,0:T(8,128)(2,1)S(1)} %spread.1) | copy-start | bytes 26738692
  148.9 3.5 %copy-start.2 = (bf16[16,272,1024]{2,1,0:T(8,128)(2,1)S(1)}, bf16[16,272,1024]{2,1,0:T(8,128)(2,1)}, u32[]{:S(2)}) copy-start(bf16[16,272,1024]{2,1,0:T(8,128)(2,1)} %copy-done.1) | copy-start | bytes 26738692
  175.0 25.5 %collective-permute-start = (bf16[2048,256]{1,0:T(8,128)(2,1)S(1)}, bf16[2048,256]{1,0:T(8,128)(2,1)S(1)}, u32[]{:S(2)}, u32[]{:S(2)}) collective-permute-start(bf16[2048,256]{1,0:T(8,128)(2,1)S(1)} %attend.2), channel_id=1, source_target_pairs={{0,16},{16,0},{1,17},{17,1},{2,18},{18,2},{3,19},{19,3},{4,20},{20... | collective-permute-start | bytes 3145736 | tf_op jit(solution)/shard_map/ppermute | solution.py:195
  199.3 1.3 copy-start.3
  199.3 25.4 %collective-permute-start.1 = (bf16[2048,256]{1,0:T(8,128)(2,1)S(1)}, bf16[2048,256]{1,0:T(8,128)(2,1)}, u32[]{:S(2)}, u32[]{:S(2)}) collective-permute-start(bf16[2048,256]{1,0:T(8,128)(2,1)S(1)} %attend.3), channel_id=1, source_target_pairs={{0,16},{16,0},{1,17},{17,1},{2,18},{18,2},{3,19},{19,3},{4,20},{20... | collective-permute-start | bytes 3145736 | tf_op jit(solution)/shard_map/ppermute | solution.py:195
  200.5 1.0 copy-start.8
  224.7 11.6 %copy-start.4 = (bf16[2048,256]{1,0:T(8,128)(2,1)S(1)}, bf16[2048,256]{1,0:T(8,128)(2,1)}, u32[]{:S(2)}) copy-start(bf16[2048,256]{1,0:T(8,128)(2,1)} %copy-done.3) | copy-start | bytes 3145732
  224.7 11.6 %copy-start.7 = (bf16[4096,2048]{1,0:T(8,128)(2,1)S(1)}, bf16[4096,2048]{1,0:T(8,128)(2,1)}, u32[]{:S(2)}) copy-start(bf16[4096,2048]{1,0:T(8,128)(2,1)} %all-gather.2.cloned.1.call-done) | copy-start | bytes 50331652
  235.7 24.5 %collective-permute-start.2 = (bf16[256,2048]{1,0:T(8,128)(2,1)S(1)}, bf16[256,2048]{1,0:T(8,128)(2,1)}, u32[]{:S(2)}, u32[]{:S(2)}) collective-permute-start(bf16[256,2048]{1,0:T(8,128)(2,1)S(1)} %convolution_convert_fusion), channel_id=1, source_target_pairs={{0,16},{16,0},{1,17},{17,1},{2,18},{18,2},{3,19},{19,3},{4,20},{20... | collective-permute-start | bytes 3145736 | tf_op jit(solution)/shard_map/ppermute | solution.py:195
Sparse Core Ops, SparseCore 0:
  9.5 180.2 all-gather.1
where the time goes:
time: 271 us
  Pallas kernels  179 us (66%)
  waiting for transfers between devices  42.3 us (16%)
  matrix products  16.5 us (6%)
  between operations  16.1 us (6%)
  local copies, waits for them, and re-layouts  14 us (5%)
  starting transfers between devices  2.75 us (1%)
    pallas_call x1, Pallas kernels, spread(): pl.pallas_call(functools.partial(spread_kernel, devices), out_shape=jax.S...  130 us
    pallas_call x2, Pallas kernels, attend(): pl.pallas_call(functools.partial(attend_kernel, half, group), out_shape=j...  45.2 us
    ppermute x3, waiting for transfers between devices, hand_on(): lax.ppermute(value, 'groups', [(i, (i + by) % parts) for i in range(parts)])  42.3 us
    dot_general x2, matrix products, project(): lax.dot_general(jnp.concatenate(rows, axis=0), weight, (((0,), (0,)), (()...  16.5 us
    unnamed x20, local copies, waits for them, and re-layouts  9.5 us
  transfers between devices with their start and end apart: 4, of which 3 were waited for; matrix products, arithmetic and copies ran while one was open for 4% of the time, Pallas kernels for 64%

commit v1 on v0

--- a/solution.py
+++ b/solution.py
@@ -224,6 +224,388 @@
     )(me_part.astype(jnp.int32).reshape(1), *results)
 
 
+def layer_kernel(sizes, first_ref, table_ref, kv_ref, q_ref, w_ref, out_ref, *scratch):
+    devices, half, kv_heads, group, head_size, share = sizes
+    (kv_all, firsts, place_vec, place_ref, w_all, acc_ref, max_ref, sum_ref, rows_ref, back_ref, *sems) = scratch
+    (far_send, far_recv, side_send, side_recv, pair_send, pair_recv) = sems[:6]
+    (wfar_send, wfar_recv, wside_send, wside_recv, wpair_send, wpair_recv) = sems[6:12]
+    (rows_send, rows_recv, back_send, back_recv, own_sem, place_sem) = sems[12:]
+    outers = devices // 4
+    blocks = 2 * devices
+    tokens = 2 * half
+    width = group * half
+    depth = kv_heads * group * head_size
+    pieces = kv_heads
+    piece = depth // pieces
+    span = BLOCKS_PER_STEP * half
+    low_groups = devices // BLOCKS_PER_STEP
+    steps = low_groups + 1
+    to_exp2 = head_size ** (-0.5) * math.log2(math.e)
+
+    part = lax.axis_index("groups")
+    me = lax.axis_index("ctx")
+    outer, middle, inner = me // 4, (me // 2) % 2, me % 2
+
+    def flip(number, by):
+        result, unit = 0, 1
+        while unit < outers:
+            result = result + (number // unit + by // unit) % 2 * unit
+            unit *= 2
+        return result
+
+    def slot_of(hop, cross, swap):
+        return (flip(outer, hop) * 2 + (middle + cross) % 2) * 2 + (inner + swap) % 2
+
+    far = [slot_of(k, 0, 0) for k in range(outers)]
+    side = slot_of(0, 1, 0)
+    pair = slot_of(0, 0, 1)
+    guest = lax.rem(part + 1, 2)
+
+    barrier = pltpu.get_barrier_semaphore()
+    for other in far[1:] + [side, pair]:
+        pl.semaphore_signal(barrier, inc=1, device_id={"ctx": other}, device_id_type=pl.DeviceIdType.MESH)
+    pl.semaphore_signal(barrier, inc=1, device_id={"groups": guest}, device_id_type=pl.DeviceIdType.MESH)
+    pl.semaphore_wait(barrier, outers + 2)
+
+    def remote(source, target, send, recv, axis, index):
+        return pltpu.make_async_remote_copy(
+            src_ref=source,
+            dst_ref=target,
+            send_sem=send,
+            recv_sem=recv,
+            device_id={axis: index},
+            device_id_type=pl.DeviceIdType.MESH,
+        )
+
+    def own_item(item):
+        return table_ref if item == 0 else kv_ref.at[pl.ds((item - 1) * half, half), :]
+
+    def item_at(item, slot):
+        if item == 0:
+            return firsts.at[slot]
+        return kv_all.at[slot * 2 + item - 1]
+
+    def source_of(item, hop, cross):
+        return own_item(item) if hop == 0 and cross == 0 else item_at(item, slot_of(hop, cross, 0))
+
+    def far_copy(item, hop):
+        return remote(own_item(item), item_at(item, me), far_send.at[item, hop], far_recv.at[item, hop], "ctx", far[hop])
+
+    def side_copy(item, hop):
+        return remote(
+            source_of(item, hop, 0), item_at(item, far[hop]), side_send.at[item, hop], side_recv.at[item, hop], "ctx", side
+        )
+
+    def pair_copy(item, hop, cross):
+        n = hop * 2 + cross
+        return remote(
+            source_of(item, hop, cross),
+            item_at(item, slot_of(hop, cross, 0)),
+            pair_send.at[item, n],
+            pair_recv.at[item, n],
+            "ctx",
+            pair,
+        )
+
+    def w_at(slot, n):
+        return w_all.at[slot, pl.ds(n * piece, piece), :]
+
+    def wfar_copy(hop, n):
+        return remote(w_at(me, n), w_at(me, n), wfar_send.at[hop, n], wfar_recv.at[hop, n], "ctx", far[hop])
+
+    def wside_copy(hop, n):
+        ref = w_at(far[hop], n)
+        return remote(ref, ref, wside_send.at[hop, n], wside_recv.at[hop, n], "ctx", side)
+
+    def wpair_copy(hop, cross, n):
+        ref = w_at(slot_of(hop, cross, 0), n)
+        return remote(ref, ref, wpair_send.at[hop * 2 + cross, n], wpair_recv.at[hop * 2 + cross, n], "ctx", pair)
+
+    def rows_copy(h):
+        cols = pl.ds(pl.multiple_of(h * piece, piece), piece)
+        return remote(
+            rows_ref.at[pl.ds(0, tokens), cols],
+            rows_ref.at[pl.ds(tokens, tokens), cols],
+            rows_send.at[h],
+            rows_recv.at[h],
+            "groups",
+            guest,
+        )
+
+    def back_copy(n, slot):
+        cols = pl.ds(pl.multiple_of((slot * 2 + part) * share, share), share)
+        return remote(back_ref.at[n], out_ref.at[:, cols], back_send.at[n], back_recv.at[n], "groups", guest)
+
+    def far_arrived(item, hop):
+        far_copy(item, hop).wait_recv()
+        side_copy(item, hop).start()
+        pair_copy(item, hop, 0).start()
+
+    def side_arrived(item, hop):
+        side_copy(item, hop).wait_recv()
+        pair_copy(item, hop, 1).start()
+
+    def pair_arrived(item, hop):
+        for cross in range(2):
+            pair_copy(item, hop, cross).wait_recv()
+
+    def wfar_arrived(hop, n):
+        wfar_copy(hop, n).wait_recv()
+        wside_copy(hop, n).start()
+        wpair_copy(hop, 0, n).start()
+
+    def wside_arrived(hop, n):
+        wside_copy(hop, n).wait_recv()
+        wpair_copy(hop, 1, n).start()
+
+    own_weight = pltpu.make_async_copy(
+        w_ref.at[:, pl.ds(pl.multiple_of(part * share, share), share)], w_all.at[me], own_sem
+    )
+    own_weight.start()
+    for item in range(3):
+        for hop in range(1, outers):
+            far_copy(item, hop).start()
+        if item < 2:
+            side_copy(item, 0).start()
+        pair_copy(item, 0, 0).start()
+    for i in range(2):
+        kv_all[me * 2 + i] = kv_ref[i * half : (i + 1) * half, :]
+    firsts[me] = table_ref[...]
+    for h in range(kv_heads):
+        max_ref[h * (steps + 1)] = jnp.full(max_ref.shape[1:], LOW_START, jnp.float32)
+        sum_ref[h * (steps + 1)] = jnp.zeros(sum_ref.shape[1:], jnp.float32)
+        acc_ref[h * (steps + 1)] = jnp.zeros(acc_ref.shape[1:], jnp.float32)
+    own_weight.wait()
+    for hop in range(1, outers):
+        for n in range(pieces):
+            wfar_copy(hop, n).start()
+
+    def step(h, which, places, old, new, reset, visible):
+        keys = pl.ds(pl.multiple_of(h * head_size, head_size), head_size)
+        values = pl.ds(pl.multiple_of((kv_heads + h) * head_size, head_size), head_size)
+        key_part = jnp.concatenate([kv_all[p, :, keys] for p in places], axis=0)
+        value_part = jnp.concatenate([kv_all[p, :, values] for p in places], axis=0)
+        scores = lax.dot_general(
+            key_part, q_ref[h, which], (((1,), (1,)), ((), ())), preferred_element_type=jnp.float32
+        )
+        old_max = max_ref[old]
+        if visible is not None:
+            scores = jnp.where(visible, scores, LOW_START)
+            old_max = jnp.where(reset, LOW_START, old_max)
+        new_max = jnp.maximum(old_max, jnp.max(scores, axis=0, keepdims=True))
+        factor = jnp.exp2((old_max - new_max) * to_exp2)
+        exp_scores = jnp.exp2((scores - new_max) * to_exp2)
+        max_ref[new] = new_max
+        sum_ref[new] = sum_ref[old] * factor + jnp.sum(exp_scores, axis=0, keepdims=True)
+        weighted = lax.dot_general(
+            value_part,
+            exp_scores.astype(jnp.bfloat16),
+            (((0,), (0,)), ((), ())),
+            preferred_element_type=jnp.float32,
+        )
+        acc_ref[new] = acc_ref[old] * factor + weighted
+
+    def low_blocks(hop):
+        start = flip(outer, hop) * 4
+
+        @pl.loop(0, kv_heads)
+        def _(h):
+            at = h * (steps + 1)
+            step(h, 1, [(start + i) * 2 for i in range(4)], at, at, None, None)
+
+    for item in range(2):
+        side_arrived(item, 0)
+        far_arrived(item, 1)
+    side_copy(2, 0).start()
+    for item in range(2):
+        pair_arrived(item, 0)
+    low_blocks(0)
+    for item in range(2):
+        for hop in range(2, outers):
+            far_arrived(item, hop)
+            side_arrived(item, hop - 1)
+        side_arrived(item, outers - 1)
+    far_arrived(2, 1)
+    side_arrived(2, 0)
+    for hop in range(1, outers):
+        for item in range(2):
+            pair_arrived(item, hop)
+        if hop == outers - 1:
+            lanes = lax.broadcasted_iota(jnp.int32, firsts.shape[1:], 1)
+            places = jnp.zeros(firsts.shape[1:], jnp.int32)
+            for d in range(devices):
+                places = places + jnp.where(firsts[d] == lanes, d * 2, 0)
+                places = places + jnp.where(blocks - 1 - firsts[d] == lanes, d * 2 + 1, 0)
+            place_vec[...] = jnp.minimum(places, blocks - 1)
+        low_blocks(hop)
+        if hop + 1 < outers:
+            far_arrived(2, hop + 1)
+        side_arrived(2, hop)
+    to_scalars = pltpu.make_async_copy(place_vec, place_ref, place_sem)
+    to_scalars.start()
+    for n in range(pieces):
+        wside_copy(0, n).start()
+        wpair_copy(0, 0, n).start()
+    for hop in range(outers):
+        pair_arrived(2, hop)
+    to_scalars.wait()
+
+    first = first_ref[0]
+    upper_steps = (devices - 1 - first) // BLOCKS_PER_STEP + 1
+    key_rows = lax.broadcasted_iota(jnp.int32, (span, width), 0)
+    query_cols = lax.broadcasted_iota(jnp.int32, (span, width), 1) % half
+
+    @pl.loop(0, kv_heads)
+    def _(h):
+        wfar_copy(1, h).wait_recv()
+        wside_copy(1, h).start()
+        wpair_copy(1, 0, h).start()
+
+        @pl.loop(0, steps)
+        def _(t):
+            upper = t < upper_steps
+            number = jnp.where(upper, low_groups + t, t - upper_steps)
+            block = jnp.where(upper, blocks - 1 - first, first)
+            which = jnp.where(upper, 1, 0)
+            places = [place_ref[0, number * BLOCKS_PER_STEP + i] for i in range(BLOCKS_PER_STEP)]
+            visible = number * span + key_rows <= block * half + query_cols
+            at = h * (steps + 1) + t
+            step(h, which, places, at, at + 1, t == upper_steps, visible)
+
+        for which in range(2):
+            at = h * (steps + 1) + (upper_steps if which == 1 else steps)
+            for g in range(group):
+                cols = pl.ds(g * half, half)
+                attended = acc_ref[at, :, cols] / sum_ref[at, :, cols]
+                target = pl.ds(pl.multiple_of(h * piece + g * head_size, head_size), head_size)
+                rows_ref[pl.ds(which * half, half), target] = attended.T.astype(jnp.bfloat16)
+        rows_copy(h).start()
+
+    for n in range(pieces):
+        wside_arrived(0, n)
+    for n in range(pieces):
+        wfar_arrived(2, n)
+    for n in range(pieces):
+        wside_arrived(1, n)
+    for h in range(kv_heads):
+        rows_copy(h).wait_recv()
+
+    def project(hop, cross):
+        n = hop * 2 + cross
+        base = slot_of(hop, cross, 0) - inner
+        for m in range(pieces):
+            wpair_copy(hop, cross, m).wait_recv()
+        weight = jnp.concatenate([w_all[base], w_all[base + 1]], axis=1)
+        product = lax.dot_general(
+            rows_ref[...], weight, (((1,), (0,)), ((), ())), preferred_element_type=jnp.float32
+        ).astype(jnp.bfloat16)
+        for i in range(2):
+            back_ref[n * 2 + i] = product[tokens:, i * share : (i + 1) * share]
+        for i in range(2):
+            cols = pl.ds(pl.multiple_of(((base + i) * 2 + part) * share, share), share)
+            out_ref[:, cols] = product[:tokens, i * share : (i + 1) * share]
+        for i in range(2):
+            back_copy(n * 2 + i, base + i).start()
+
+    project(0, 0)
+    project(0, 1)
+    for n in range(pieces):
+        wfar_arrived(3, n)
+    for n in range(pieces):
+        wside_arrived(2, n)
+    project(1, 0)
+    project(1, 1)
+    project(2, 0)
+    project(2, 1)
+    for n in range(pieces):
+        wside_arrived(3, n)
+    project(3, 0)
+    project(3, 1)
+
+    for n in range(2 * 2 * outers):
+        back_copy(n, 0).wait_recv()
+    for n in range(2 * 2 * outers):
+        back_copy(n, 0).wait_send()
+    for h in range(kv_heads):
+        rows_copy(h).wait_send()
+    for hop in range(outers):
+        for item in range(3):
+            if hop:
+                far_copy(item, hop).wait_send()
+            side_copy(item, hop).wait_send()
+            for cross in range(2):
+                pair_copy(item, hop, cross).wait_send()
+        for n in range(pieces):
+            if hop:
+                wfar_copy(hop, n).wait_send()
+            wside_copy(hop, n).wait_send()
+            for cross in range(2):
+                wpair_copy(hop, cross, n).wait_send()
+
+
+def layer(query_parts, packed, first, out_weight, half):
+    devices = lax.axis_size("ctx")
+    outers = devices // 4
+    kv_heads, _, width, head_size = query_parts.shape
+    group = width // half
+    tokens = 2 * half
+    depth, columns = out_weight.shape
+    share = columns // 2
+    steps = devices // BLOCKS_PER_STEP + 1
+    slots = kv_heads * (steps + 1)
+    pieces = kv_heads
+    table = jnp.full((8, 128), first, jnp.int32)
+    dma = pltpu.SemaphoreType.DMA
+    flops = 4 * query_parts.size * half * (2 * devices + 1) // 2 + 4 * tokens * depth * columns * devices // 2
+    return pl.pallas_call(
+        functools.partial(layer_kernel, (devices, half, kv_heads, group, head_size, share)),
+        out_shape=jax.ShapeDtypeStruct((tokens, columns * devices), jnp.bfloat16),
+        in_specs=[
+            pl.BlockSpec(memory_space=pltpu.SMEM),
+            pl.BlockSpec(memory_space=pltpu.VMEM),
+            pl.BlockSpec(memory_space=pltpu.VMEM),
+            pl.BlockSpec(memory_space=pltpu.VMEM),
+            pl.BlockSpec(memory_space=pl.ANY),
+        ],
+        out_specs=pl.BlockSpec(memory_space=pltpu.VMEM),
+        scratch_shapes=[
+            pltpu.VMEM((2 * devices, half, packed.shape[1]), packed.dtype),
+            pltpu.VMEM((devices, 8, 128), jnp.int32),
+            pltpu.VMEM((8, 128), jnp.int32),
+            pltpu.SMEM((8, 128), jnp.int32),
+            pltpu.VMEM((devices, depth, share), out_weight.dtype),
+            pltpu.VMEM((slots, head_size, width), jnp.float32),
+            pltpu.VMEM((slots, 1, width), jnp.float32),
+            pltpu.VMEM((slots, 1, width), jnp.float32),
+            pltpu.VMEM((2 * tokens, depth), jnp.bfloat16),
+            pltpu.VMEM((devices, tokens, share), jnp.bfloat16),
+            dma((3, outers)),
+            dma((3, outers)),
+            dma((3, outers)),
+            dma((3, outers)),
+            dma((3, 2 * outers)),
+            dma((3, 2 * outers)),
+            dma((outers, pieces)),
+            dma((outers, pieces)),
+            dma((outers, pieces)),
+            dma((outers, pieces)),
+            dma((2 * outers, pieces)),
+            dma((2 * outers, pieces)),
+            dma((kv_heads,)),
+            dma((kv_heads,)),
+            dma((devices,)),
+            dma((devices,)),
+            dma,
+            dma,
+        ],
+        compiler_params=pltpu.CompilerParams(
+            collective_id=0, has_side_effects=True, vmem_limit_bytes=60 * 1024 * 1024
+        ),
+        cost_estimate=pl.CostEstimate(flops=flops, bytes_accessed=2 * out_weight.size, transcendentals=0),
+        name="layer",
+    )(first.reshape(1), table, packed, query_parts, out_weight)
+
+
 def local(query_states, key_states, value_rows, positions, out_weight):
     tokens, query_heads, head_size = query_states.shape
     kv_heads = key_states.shape[1]
@@ -234,6 +616,13 @@
     parts = lax.axis_size("groups")
     me_part = lax.axis_index("groups")
     share = out_weight.shape[1] // parts
+    query_parts = query_states.reshape(2, half, kv_heads, group, head_size).transpose(2, 0, 3, 1, 4)
+    query_parts = query_parts.reshape(kv_heads, 2, group * half, head_size)
+    if parts == 2 and lax.axis_size("tp") == 1 and devices == 4 * BLOCKS_PER_STEP and share % 128 == 0:
+        packed = jnp.concatenate(
+            [key_states.reshape(tokens, kv_heads * head_size), value_rows.reshape(tokens, kv_heads * head_size)], axis=1
+        )
+        return layer(query_parts, packed, positions[0] // half, out_weight, half)
     weight_share = lax.dynamic_slice_in_dim(out_weight, me_part * share, share, 1)
     weight = lax.all_gather(weight_share, "ctx", axis=1, tiled=True)
     packed = jnp.concatenate(
@@ -251,8 +640,6 @@
     place = jnp.sum(jnp.where(stored == wanted, starts, 0), axis=1)
     place = place.astype(jnp.int32)
     own = jnp.stack([first, blocks - 1 - first]).astype(jnp.int32)
-    query_parts = query_states.reshape(2, half, kv_heads, group, head_size).transpose(2, 0, 3, 1, 4)
-    query_parts = query_parts.reshape(kv_heads, 2, group * half, head_size)
     pieces = min(2, kv_heads)
     span = kv_heads // pieces
     attended = [

time: 271 us -> 178 us (0.66)
  the two profiles are of different devices: /device:TPU:24 before, /device:TPU:0 now
where the time goes in v1:
time: 178 us
  Pallas kernels  166 us (93%)
  local copies, waits for them, and re-layouts  8.29 us (5%)
  between operations  2.62 us (1%)
    pallas_call x1, Pallas kernels, layer(): pl.pallas_call(functools.partial(layer_kernel, (devices, half, kv_heads,...  166 us

profile of v1, /device:TPU:0, one launch (start us, length us, event | category | flops | bytes accessed | tf_op | source)
XLA Modules:
  0.0 177.8 jit_solution(8590554029325533286)
XLA Ops:
  0.0 0.0 copy-start
  0.0 1.3 slice.3
  3.9 0.6 broadcast_in_dim.3.table_ref
  4.5 1.1 copy_bitcast_fusion
  5.6 0.9 pad_maximum_fusion.kv_ref
  6.5 0.0 copy-done
  6.5 2.1 %copy.6 = bf16[2,128,4,8,128]{4,1,3,0,2:T(8,128)(2,1)} copy(bf16[2,128,4,8,128]{4,3,2,1,0:T(8,128)(2,1)S(1)} %bitcast.12) | data formatting | bytes 4194304 | tf_op jit(solution)/shard_map/reshape | solution.py:619
  8.6 166.1 %layer.1 = bf16[256,4096]{1,0:T(8,128)(2,1)} custom-call(s32[1]{0:T(128)} %bitcast.1.first_ref, s32[8,128]{1,0:T(8,128)} %broadcast_in_dim.3.table_ref, bf16[256,1024]{1,0:T(8,128)(2,1)} %pad_maximum_fusion.kv_ref, bf16[4,2,1024,128]{3,2,1,0:T(8,128)(2,1)} %bitcast.13, bf16[4096,256]{1,0:T(8,128)(2,1)} %w_ref.1), custom_call_target="tpu_custom_call" | custom-call | flops 17448304640 | bytes 2097152 | tf_op jit(solution)/shard_map/layer/pallas_call | solution.py:560
  174.7 3.1 %copy.12 = bf16[256,4096]{1,0:T(8,128)(2,1)} copy(bf16[256,4096]{1,0:T(8,128)(2,1)} %layer.1) | data formatting | bytes 4194304
Async XLA Ops:
  0.0 6.5 %copy-start = (bf16[256,32,128]{2,1,0:T(8,128)(2,1)S(1)}, bf16[256,32,128]{2,1,0:T(8,128)(2,1)}, u32[]{:S(2)}) copy-start(bf16[256,32,128]{2,1,0:T(8,128)(2,1)} %param.5) | copy-start | bytes 6291460

commit v2 on v1

--- a/solution.py
+++ b/solution.py
@@ -12,6 +12,7 @@
 BLOCKS_PER_STEP = 4
 CHUNK = 1024
 TAIL = 16
+VMEM = 50 * 1024 * 1024
 
 
 def attend_kernel(half, group, place_ref, own_ref, q_ref, k_ref, v_ref, out_ref, acc_ref, max_ref, sum_ref):
@@ -226,10 +227,10 @@
 
 def layer_kernel(sizes, first_ref, table_ref, kv_ref, q_ref, w_ref, out_ref, *scratch):
     devices, half, kv_heads, group, head_size, share = sizes
-    (kv_all, firsts, place_vec, place_ref, w_all, acc_ref, max_ref, sum_ref, rows_ref, back_ref, *sems) = scratch
+    (kv_low, kv_high, firsts, place_vec, place_ref, w_all, acc_ref, max_ref, sum_ref, rows_ref, back_ref, *sems) = scratch
     (far_send, far_recv, side_send, side_recv, pair_send, pair_recv) = sems[:6]
     (wfar_send, wfar_recv, wside_send, wside_recv, wpair_send, wpair_recv) = sems[6:12]
-    (rows_send, rows_recv, back_send, back_recv, own_sem, place_sem) = sems[12:]
+    (rows_send, rows_recv, back_send, back_recv, pass_send, wpass_send, own_sem, place_sem) = sems[12:]
     outers = devices // 4
     blocks = 2 * devices
     tokens = 2 * half
@@ -238,8 +239,7 @@
     pieces = kv_heads
     piece = depth // pieces
     span = BLOCKS_PER_STEP * half
-    low_groups = devices // BLOCKS_PER_STEP
-    steps = low_groups + 1
+    groups = devices // BLOCKS_PER_STEP
     to_exp2 = head_size ** (-0.5) * math.log2(math.e)
 
     part = lax.axis_index("groups")
@@ -259,6 +259,8 @@
     far = [slot_of(k, 0, 0) for k in range(outers)]
     side = slot_of(0, 1, 0)
     pair = slot_of(0, 0, 1)
+    inside = jnp.logical_and(outer > 0, outer < outers - 1)
+    last = pieces - 1
     guest = lax.rem(part + 1, 2)
 
     barrier = pltpu.get_barrier_semaphore()
@@ -283,13 +285,17 @@
     def item_at(item, slot):
         if item == 0:
             return firsts.at[slot]
-        return kv_all.at[slot * 2 + item - 1]
+        return (kv_low if item == 1 else kv_high).at[slot]
 
     def source_of(item, hop, cross):
         return own_item(item) if hop == 0 and cross == 0 else item_at(item, slot_of(hop, cross, 0))
 
     def far_copy(item, hop):
         return remote(own_item(item), item_at(item, me), far_send.at[item, hop], far_recv.at[item, hop], "ctx", far[hop])
+
+    def pass_copy(item):
+        ref = item_at(item, far[2])
+        return remote(ref, ref, pass_send.at[item], far_recv.at[item, 3], "ctx", far[1])
 
     def side_copy(item, hop):
         return remote(
@@ -310,8 +316,16 @@
     def w_at(slot, n):
         return w_all.at[slot, pl.ds(n * piece, piece), :]
 
-    def wfar_copy(hop, n):
-        return remote(w_at(me, n), w_at(me, n), wfar_send.at[hop, n], wfar_recv.at[hop, n], "ctx", far[hop])
+    def far_part(hop, e):
+        return w_at(slot_of(hop, 0, 0), e) if e < pieces else w_at(slot_of(hop, 1, 0), last)
+
+    def wfar_copy(hop, e):
+        ref = far_part(0, e)
+        return remote(ref, ref, wfar_send.at[hop, e], wfar_recv.at[hop, e], "ctx", far[hop])
+
+    def wpass_copy(e):
+        ref = far_part(2, e)
+        return remote(ref, ref, wpass_send.at[e], wfar_recv.at[3, e], "ctx", far[1])
 
     def wside_copy(hop, n):
         ref = w_at(far[hop], n)
@@ -321,13 +335,13 @@
         ref = w_at(slot_of(hop, cross, 0), n)
         return remote(ref, ref, wpair_send.at[hop * 2 + cross, n], wpair_recv.at[hop * 2 + cross, n], "ctx", pair)
 
-    def rows_copy(h):
+    def rows_copy(which, h):
         cols = pl.ds(pl.multiple_of(h * piece, piece), piece)
         return remote(
-            rows_ref.at[pl.ds(0, tokens), cols],
-            rows_ref.at[pl.ds(tokens, tokens), cols],
-            rows_send.at[h],
-            rows_recv.at[h],
+            rows_ref.at[pl.ds(which * half, half), cols],
+            rows_ref.at[pl.ds(tokens + which * half, half), cols],
+            rows_send.at[which, h],
+            rows_recv.at[which, h],
             "groups",
             guest,
         )
@@ -336,8 +350,25 @@
         cols = pl.ds(pl.multiple_of((slot * 2 + part) * share, share), share)
         return remote(back_ref.at[n], out_ref.at[:, cols], back_send.at[n], back_recv.at[n], "groups", guest)
 
+    def far_start(copy, hop):
+        if hop == 3:
+
+            @pl.when(inside)
+            def _():
+                copy.start()
+
+        else:
+            copy.start()
+
+    def pass_on(copy):
+        @pl.when(inside)
+        def _():
+            copy.start()
+
     def far_arrived(item, hop):
         far_copy(item, hop).wait_recv()
+        if hop == 2:
+            pass_on(pass_copy(item))
         side_copy(item, hop).start()
         pair_copy(item, hop, 0).start()
 
@@ -349,10 +380,13 @@
         for cross in range(2):
             pair_copy(item, hop, cross).wait_recv()
 
-    def wfar_arrived(hop, n):
-        wfar_copy(hop, n).wait_recv()
-        wside_copy(hop, n).start()
-        wpair_copy(hop, 0, n).start()
+    def wfar_arrived(hop, e):
+        wfar_copy(hop, e).wait_recv()
+        if hop == 2:
+            pass_on(wpass_copy(e))
+        if e < last:
+            wside_copy(hop, e).start()
+        wpair_copy(hop, 1 if e == pieces else 0, min(e, last)).start()
 
     def wside_arrived(hop, n):
         wside_copy(hop, n).wait_recv()
@@ -362,133 +396,181 @@
         w_ref.at[:, pl.ds(pl.multiple_of(part * share, share), share)], w_all.at[me], own_sem
     )
     own_weight.start()
-    for item in range(3):
+    def own_start(item):
         for hop in range(1, outers):
-            far_copy(item, hop).start()
-        if item < 2:
-            side_copy(item, 0).start()
+            far_start(far_copy(item, hop), hop)
+
+    for item in range(2):
+        side_copy(item, 0).start()
+        own_start(item)
         pair_copy(item, 0, 0).start()
-    for i in range(2):
-        kv_all[me * 2 + i] = kv_ref[i * half : (i + 1) * half, :]
+    pair_copy(2, 0, 0).start()
+    kv_low[me] = kv_ref[:half, :]
+    kv_high[me] = kv_ref[half:, :]
     firsts[me] = table_ref[...]
+
+    def clear(at):
+        max_ref[at] = jnp.full(max_ref.shape[1:], LOW_START, jnp.float32)
+        sum_ref[at] = jnp.zeros(sum_ref.shape[1:], jnp.float32)
+        acc_ref[at] = jnp.zeros(acc_ref.shape[1:], jnp.float32)
+
     for h in range(kv_heads):
-        max_ref[h * (steps + 1)] = jnp.full(max_ref.shape[1:], LOW_START, jnp.float32)
-        sum_ref[h * (steps + 1)] = jnp.zeros(sum_ref.shape[1:], jnp.float32)
-        acc_ref[h * (steps + 1)] = jnp.zeros(acc_ref.shape[1:], jnp.float32)
+        clear(h)
     own_weight.wait()
-    for hop in range(1, outers):
-        for n in range(pieces):
-            wfar_copy(hop, n).start()
-
-    def step(h, which, places, old, new, reset, visible):
+
+    def step(h, which, source, places, at, visible):
         keys = pl.ds(pl.multiple_of(h * head_size, head_size), head_size)
         values = pl.ds(pl.multiple_of((kv_heads + h) * head_size, head_size), head_size)
-        key_part = jnp.concatenate([kv_all[p, :, keys] for p in places], axis=0)
-        value_part = jnp.concatenate([kv_all[p, :, values] for p in places], axis=0)
+        key_part = jnp.concatenate([source[p, :, keys] for p in places], axis=0)
+        value_part = jnp.concatenate([source[p, :, values] for p in places], axis=0)
         scores = lax.dot_general(
             key_part, q_ref[h, which], (((1,), (1,)), ((), ())), preferred_element_type=jnp.float32
         )
-        old_max = max_ref[old]
+        old_max = max_ref[at]
         if visible is not None:
             scores = jnp.where(visible, scores, LOW_START)
-            old_max = jnp.where(reset, LOW_START, old_max)
         new_max = jnp.maximum(old_max, jnp.max(scores, axis=0, keepdims=True))
         factor = jnp.exp2((old_max - new_max) * to_exp2)
         exp_scores = jnp.exp2((scores - new_max) * to_exp2)
-        max_ref[new] = new_max
-        sum_ref[new] = sum_ref[old] * factor + jnp.sum(exp_scores, axis=0, keepdims=True)
+        max_ref[at] = new_max
+        sum_ref[at] = sum_ref[at] * factor + jnp.sum(exp_scores, axis=0, keepdims=True)
         weighted = lax.dot_general(
             value_part,
             exp_scores.astype(jnp.bfloat16),
             (((0,), (0,)), ((), ())),
             preferred_element_type=jnp.float32,
         )
-        acc_ref[new] = acc_ref[old] * factor + weighted
-
-    def low_blocks(hop):
+        acc_ref[at] = acc_ref[at] * factor + weighted
+
+    def run_hooks(number, hooks):
+        for at, actions in hooks.items():
+
+            @pl.when(number == at)
+            def _():
+                for action in actions:
+                    action()
+
+    def low_blocks(hop, hooks):
         start = flip(outer, hop) * 4
 
         @pl.loop(0, kv_heads)
         def _(h):
-            at = h * (steps + 1)
-            step(h, 1, [(start + i) * 2 for i in range(4)], at, at, None, None)
-
-    for item in range(2):
-        side_arrived(item, 0)
-        far_arrived(item, 1)
-    side_copy(2, 0).start()
-    for item in range(2):
-        pair_arrived(item, 0)
-    low_blocks(0)
-    for item in range(2):
-        for hop in range(2, outers):
+            run_hooks(h, hooks)
+            step(h, 1, kv_low, [start + i for i in range(4)], h, None)
+
+    def low_side(hop):
+        for item in range(2):
+            side_arrived(item, hop)
+
+    def low_far(hop):
+        for item in range(2):
             far_arrived(item, hop)
-            side_arrived(item, hop - 1)
-        side_arrived(item, outers - 1)
-    far_arrived(2, 1)
-    side_arrived(2, 0)
-    for hop in range(1, outers):
+
+    def low_pair(hop):
         for item in range(2):
             pair_arrived(item, hop)
-        if hop == outers - 1:
-            lanes = lax.broadcasted_iota(jnp.int32, firsts.shape[1:], 1)
-            places = jnp.zeros(firsts.shape[1:], jnp.int32)
-            for d in range(devices):
-                places = places + jnp.where(firsts[d] == lanes, d * 2, 0)
-                places = places + jnp.where(blocks - 1 - firsts[d] == lanes, d * 2 + 1, 0)
-            place_vec[...] = jnp.minimum(places, blocks - 1)
-        low_blocks(hop)
-        if hop + 1 < outers:
-            far_arrived(2, hop + 1)
-        side_arrived(2, hop)
+
+    def weight_round(e):
+        for hop in (2, 1, 3):
+            far_start(wfar_copy(hop, e), hop)
+
+    def weight_own(n):
+        wside_copy(0, n).start()
+        wpair_copy(0, 0, n).start()
+
+    def do(action, *args):
+        return functools.partial(action, *args)
+
+    low_side(0)
+    low_pair(0)
+    low_blocks(0, {2: [do(low_far, 1)], 3: [do(own_start, 2)]})
+    low_far(2)
+    low_side(1)
+    low_pair(1)
+    low_blocks(1, {0: [side_copy(2, 0).start], 2: [do(low_far, 3)]})
+    low_side(2)
+    low_pair(2)
+    low_blocks(2, {1: [do(far_arrived, 2, 1)], 3: [do(far_arrived, 2, 2), do(weight_round, 0)]})
+    low_side(3)
+    low_pair(3)
+    lanes = lax.broadcasted_iota(jnp.int32, firsts.shape[1:], 1)
+    numbers = jnp.zeros(firsts.shape[1:], jnp.int32)
+    for d in range(devices):
+        numbers = numbers + jnp.where(firsts[d] == lanes, d, 0)
+        numbers = numbers + jnp.where(blocks - 1 - firsts[d] == lanes, d, 0)
+    place_vec[...] = jnp.minimum(numbers, devices - 1)
+    low_blocks(3, {0: [do(side_arrived, 2, 0)], 1: [do(weight_own, last)], 3: [do(far_arrived, 2, 3)]})
     to_scalars = pltpu.make_async_copy(place_vec, place_ref, place_sem)
     to_scalars.start()
-    for n in range(pieces):
-        wside_copy(0, n).start()
-        wpair_copy(0, 0, n).start()
-    for hop in range(outers):
-        pair_arrived(2, hop)
     to_scalars.wait()
 
     first = first_ref[0]
-    upper_steps = (devices - 1 - first) // BLOCKS_PER_STEP + 1
     key_rows = lax.broadcasted_iota(jnp.int32, (span, width), 0)
     query_cols = lax.broadcasted_iota(jnp.int32, (span, width), 1) % half
 
-    @pl.loop(0, kv_heads)
-    def _(h):
-        wfar_copy(1, h).wait_recv()
-        wside_copy(1, h).start()
-        wpair_copy(1, 0, h).start()
-
-        @pl.loop(0, steps)
-        def _(t):
-            upper = t < upper_steps
-            number = jnp.where(upper, low_groups + t, t - upper_steps)
-            block = jnp.where(upper, blocks - 1 - first, first)
-            which = jnp.where(upper, 1, 0)
-            places = [place_ref[0, number * BLOCKS_PER_STEP + i] for i in range(BLOCKS_PER_STEP)]
-            visible = number * span + key_rows <= block * half + query_cols
-            at = h * (steps + 1) + t
-            step(h, which, places, at, at + 1, t == upper_steps, visible)
-
-        for which in range(2):
-            at = h * (steps + 1) + (upper_steps if which == 1 else steps)
+    def finish(which, hooks):
+        block = blocks - 1 - first if which else first
+
+        @pl.loop(0, kv_heads)
+        def _(h):
+            at = h if which else kv_heads
+            if not which:
+                clear(at)
+
+            @pl.loop(0, groups)
+            def _(t):
+                run_hooks(h * groups + t, hooks)
+
+                @pl.when(jnp.logical_and(t == 1, h > 0))
+                def _():
+                    rows_copy(which, h - 1).start()
+
+                number = groups + t if which else t
+                places = [place_ref[0, number * BLOCKS_PER_STEP + i] for i in range(BLOCKS_PER_STEP)]
+                visible = number * span + key_rows <= block * half + query_cols
+                step(h, which, kv_high if which else kv_low, places, at, visible)
+
             for g in range(group):
                 cols = pl.ds(g * half, half)
                 attended = acc_ref[at, :, cols] / sum_ref[at, :, cols]
                 target = pl.ds(pl.multiple_of(h * piece + g * head_size, head_size), head_size)
                 rows_ref[pl.ds(which * half, half), target] = attended.T.astype(jnp.bfloat16)
-        rows_copy(h).start()
-
-    for n in range(pieces):
-        wside_arrived(0, n)
-    for n in range(pieces):
-        wfar_arrived(2, n)
-    for n in range(pieces):
-        wside_arrived(1, n)
-    for h in range(kv_heads):
-        rows_copy(h).wait_recv()
+
+    finish(
+        0,
+        {
+            0: [do(side_arrived, 2, 1), do(weight_own, 0)],
+            1: [do(weight_round, 1)],
+            4: [do(side_arrived, 2, 2)],
+            5: [do(weight_own, 1)],
+            8: [do(side_arrived, 2, 3), do(weight_own, 2)],
+            10: [do(wfar_arrived, 1, 0)],
+            11: [do(wfar_arrived, 2, 0)],
+            12: [do(weight_round, 2)],
+        },
+    )
+    for hop in range(outers):
+        pair_arrived(2, hop)
+    rows_copy(0, kv_heads - 1).start()
+    finish(
+        1,
+        {
+            1: [do(wside_arrived, 0, last)],
+            2: [do(wfar_arrived, 3, 0)],
+            3: [do(weight_round, last)],
+            4: [do(wfar_arrived, 1, 1)],
+            5: [do(wside_arrived, 0, 0)],
+            7: [do(wfar_arrived, 2, 1)],
+            9: [do(wside_arrived, 0, 1)],
+            11: [do(weight_round, pieces)],
+            12: [do(wfar_arrived, 1, 2)],
+            13: [do(wfar_arrived, 3, 1)],
+            14: [do(wside_arrived, 0, 2)],
+            15: [do(wfar_arrived, 2, 2), do(wside_arrived, 1, 0)],
+        },
+    )
+    wside_arrived(2, 0)
+    rows_copy(1, kv_heads - 1).start()
 
     def project(hop, cross):
         n = hop * 2 + cross
@@ -507,40 +589,63 @@
         for i in range(2):
             back_copy(n * 2 + i, base + i).start()
 
+    wfar_arrived(3, 2)
+    wside_arrived(3, 0)
+    for which in range(2):
+        for h in range(kv_heads):
+            rows_copy(which, h).wait_recv()
+    wside_arrived(1, 1)
     project(0, 0)
+    wfar_arrived(1, last)
+    wfar_arrived(2, last)
     project(0, 1)
-    for n in range(pieces):
-        wfar_arrived(3, n)
-    for n in range(pieces):
-        wside_arrived(2, n)
+    wside_arrived(2, 1)
+    wfar_arrived(1, pieces)
+    wfar_arrived(2, pieces)
+    wside_arrived(3, 1)
     project(1, 0)
+    wside_arrived(1, 2)
     project(1, 1)
+    wfar_arrived(3, last)
     project(2, 0)
+    wside_arrived(2, 2)
     project(2, 1)
-    for n in range(pieces):
-        wside_arrived(3, n)
+    wfar_arrived(3, pieces)
     project(3, 0)
+    wside_arrived(3, 2)
     project(3, 1)
 
     for n in range(2 * 2 * outers):
         back_copy(n, 0).wait_recv()
     for n in range(2 * 2 * outers):
         back_copy(n, 0).wait_send()
-    for h in range(kv_heads):
-        rows_copy(h).wait_send()
+    for which in range(2):
+        for h in range(kv_heads):
+            rows_copy(which, h).wait_send()
     for hop in range(outers):
         for item in range(3):
-            if hop:
+            if 0 < hop < 3:
                 far_copy(item, hop).wait_send()
             side_copy(item, hop).wait_send()
             for cross in range(2):
                 pair_copy(item, hop, cross).wait_send()
         for n in range(pieces):
-            if hop:
-                wfar_copy(hop, n).wait_send()
-            wside_copy(hop, n).wait_send()
+            if hop == 0 or n < last:
+                wside_copy(hop, n).wait_send()
             for cross in range(2):
                 wpair_copy(hop, cross, n).wait_send()
+        for e in range(pieces + 1):
+            if 0 < hop < 3:
+                wfar_copy(hop, e).wait_send()
+
+    @pl.when(inside)
+    def _():
+        for item in range(3):
+            far_copy(item, 3).wait_send()
+            pass_copy(item).wait_send()
+        for e in range(pieces + 1):
+            wfar_copy(3, e).wait_send()
+            wpass_copy(e).wait_send()
 
 
 def layer(query_parts, packed, first, out_weight, half):
@@ -551,8 +656,7 @@
     tokens = 2 * half
     depth, columns = out_weight.shape
     share = columns // 2
-    steps = devices // BLOCKS_PER_STEP + 1
-    slots = kv_heads * (steps + 1)
+    slots = kv_heads + 1
     pieces = kv_heads
     table = jnp.full((8, 128), first, jnp.int32)
     dma = pltpu.SemaphoreType.DMA
@@ -569,7 +673,8 @@
         ],
         out_specs=pl.BlockSpec(memory_space=pltpu.VMEM),
         scratch_shapes=[
-            pltpu.VMEM((2 * devices, half, packed.shape[1]), packed.dtype),
+            pltpu.VMEM((devices, half, packed.shape[1]), packed.dtype),
+            pltpu.VMEM((devices, half, packed.shape[1]), packed.dtype),
             pltpu.VMEM((devices, 8, 128), jnp.int32),
             pltpu.VMEM((8, 128), jnp.int32),
             pltpu.SMEM((8, 128), jnp.int32),
@@ -585,21 +690,23 @@
             dma((3, outers)),
             dma((3, 2 * outers)),
             dma((3, 2 * outers)),
-            dma((outers, pieces)),
-            dma((outers, pieces)),
+            dma((outers, pieces + 1)),
+            dma((outers, pieces + 1)),
             dma((outers, pieces)),
             dma((outers, pieces)),
             dma((2 * outers, pieces)),
             dma((2 * outers, pieces)),
-            dma((kv_heads,)),
-            dma((kv_heads,)),
+            dma((2, kv_heads)),
+            dma((2, kv_heads)),
             dma((devices,)),
             dma((devices,)),
+            dma((3,)),
+            dma((pieces + 1,)),
             dma,
             dma,
         ],
         compiler_params=pltpu.CompilerParams(
-            collective_id=0, has_side_effects=True, vmem_limit_bytes=60 * 1024 * 1024
+            collective_id=0, has_side_effects=True, vmem_limit_bytes=VMEM
         ),
         cost_estimate=pl.CostEstimate(flops=flops, bytes_accessed=2 * out_weight.size, transcendentals=0),
         name="layer",

time: 178 us -> 159 us (0.89)
  Pallas kernels: 166 us -> 150 us
  local copies, waits for them, and re-layouts: 8.29 us -> 5.89 us
    pallas_call x1, Pallas kernels: 166 us -> 150 us  [layer(): pl.pallas_call(functools.partial(layer_kernel, (devices, half, kv_heads,...]
    unnamed x3, local copies, waits for them, and re-layouts: 3.13 us -> 1.33 us
where the time goes in v2:
time: 159 us
  Pallas kernels  150 us (94%)
  local copies, waits for them, and re-layouts  5.89 us (4%)
  between operations  2.64 us (2%)
    pallas_call x1, Pallas kernels, layer(): pl.pallas_call(functools.partial(layer_kernel, (devices, half, kv_heads,...  150 us

profile of v2, /device:TPU:0, one launch (start us, length us, event | category | flops | bytes accessed | tf_op | source)
XLA Modules:
  0.0 158.7 jit_solution(14199728908168715755)
XLA Ops:
  0.0 0.0 copy-start
  0.0 1.3 slice.3
  4.0 1.1 copy_bitcast_fusion
  5.1 0.1 pad_maximum_fusion.kv_ref
  5.1 0.0 copy-done
  5.1 2.1 %copy.6 = bf16[2,128,4,8,128]{4,1,3,0,2:T(8,128)(2,1)} copy(bf16[2,128,4,8,128]{4,3,2,1,0:T(8,128)(2,1)S(1)} %bitcast.12) | data formatting | bytes 4194304 | tf_op jit(solution)/shard_map/reshape | solution.py:726
  7.3 150.1 %layer.1 = bf16[256,4096]{1,0:T(8,128)(2,1)S(1)} custom-call(s32[1]{0:T(128)} %bitcast.1.first_ref, s32[8,128]{1,0:T(8,128)S(1)} %broadcast_in_dim.3.table_ref, bf16[256,1024]{1,0:T(8,128)(2,1)S(1)} %pad_maximum_fusion.kv_ref, bf16[4,2,1024,128]{3,2,1,0:T(8,128)(2,1)} %bitcast.13, bf16[4096,256]{1,0:T(8,128)(2,1)} %w_ref.1), custom_call_target="tpu_custom_call" | custom-call | flops 17448304640 | bytes 2097152 | tf_op jit(solution)/shard_map/layer/pallas_call | solution.py:664
  157.3 1.3 copy.12
  (1 shorter events, 0.0 us)
Async XLA Ops:
  0.0 5.1 %copy-start = (bf16[256,32,128]{2,1,0:T(8,128)(2,1)S(1)}, bf16[256,32,128]{2,1,0:T(8,128)(2,1)}, u32[]{:S(2)}) copy-start(bf16[256,32,128]{2,1,0:T(8,128)(2,1)} %param.5) | copy-start | bytes 6291460

commit v3 on v2

--- a/solution.py
+++ b/solution.py
@@ -225,12 +225,12 @@
     )(me_part.astype(jnp.int32).reshape(1), *results)
 
 
-def layer_kernel(sizes, first_ref, table_ref, kv_ref, q_ref, w_ref, out_ref, *scratch):
+def layer_kernel(sizes, order_ref, table_ref, kv_ref, q_raw, w_ref, out_ref, *scratch):
     devices, half, kv_heads, group, head_size, share = sizes
-    (kv_low, kv_high, firsts, place_vec, place_ref, w_all, acc_ref, max_ref, sum_ref, rows_ref, back_ref, *sems) = scratch
+    (kv_low, kv_high, firsts, place_vec, place_ref, w_all, acc_ref, max_ref, sum_ref, rows_ref, back_ref, part_ref, q_in, q_ref, turn_ref, *sems) = scratch
     (far_send, far_recv, side_send, side_recv, pair_send, pair_recv) = sems[:6]
     (wfar_send, wfar_recv, wside_send, wside_recv, wpair_send, wpair_recv) = sems[6:12]
-    (rows_send, rows_recv, back_send, back_recv, pass_send, wpass_send, own_sem, place_sem) = sems[12:]
+    (rows_send, rows_recv, back_send, back_recv, pass_send, wpass_send, own_sem, place_sem, q_sem) = sems[12:]
     outers = devices // 4
     blocks = 2 * devices
     tokens = 2 * half
@@ -396,6 +396,8 @@
         w_ref.at[:, pl.ds(pl.multiple_of(part * share, share), share)], w_all.at[me], own_sem
     )
     own_weight.start()
+    queries = pltpu.make_async_copy(q_raw, q_in, q_sem)
+    queries.start()
     def own_start(item):
         for hop in range(1, outers):
             far_start(far_copy(item, hop), hop)
@@ -416,6 +418,11 @@
 
     for h in range(kv_heads):
         clear(h)
+    queries.wait()
+    for h in range(kv_heads):
+        for which in range(2):
+            mine = q_in[which * half : (which + 1) * half, h * group : (h + 1) * group, :]
+            q_ref[h, which] = mine.reshape(width, head_size)
     own_weight.wait()
 
     def step(h, which, source, places, at, visible):
@@ -450,13 +457,16 @@
                 for action in actions:
                     action()
 
-    def low_blocks(hop, hooks):
-        start = flip(outer, hop) * 4
+    def low_blocks(parts, hooks):
+        places = [slot_of(hop, cross, swap) for hop, cross in parts for swap in range(2)]
+        for hop, cross in parts:
+            for item in range(2):
+                pair_copy(item, hop, cross).wait_recv()
 
         @pl.loop(0, kv_heads)
         def _(h):
             run_hooks(h, hooks)
-            step(h, 1, kv_low, [start + i for i in range(4)], h, None)
+            step(h, 1, kv_low, places, h, None)
 
     def low_side(hop):
         for item in range(2):
@@ -466,10 +476,6 @@
         for item in range(2):
             far_arrived(item, hop)
 
-    def low_pair(hop):
-        for item in range(2):
-            pair_arrived(item, hop)
-
     def weight_round(e):
         for hop in (2, 1, 3):
             far_start(wfar_copy(hop, e), hop)
@@ -482,31 +488,33 @@
         return functools.partial(action, *args)
 
     low_side(0)
-    low_pair(0)
-    low_blocks(0, {2: [do(low_far, 1)], 3: [do(own_start, 2)]})
+    low_blocks([(0, 0), (0, 1)], {3: [do(low_far, 1)]})
     low_far(2)
+    own_start(2)
+    low_blocks([(1, 0), (2, 0)], {2: [side_copy(2, 0).start]})
     low_side(1)
-    low_pair(1)
-    low_blocks(1, {0: [side_copy(2, 0).start], 2: [do(low_far, 3)]})
-    low_side(2)
-    low_pair(2)
-    low_blocks(2, {1: [do(far_arrived, 2, 1)], 3: [do(far_arrived, 2, 2), do(weight_round, 0)]})
+    low_far(3)
+    low_blocks([(1, 1), (3, 0)], {1: [do(low_side, 2)], 3: [do(far_arrived, 2, 1)]})
+    far_arrived(2, 2)
+    weight_round(0)
     low_side(3)
-    low_pair(3)
-    lanes = lax.broadcasted_iota(jnp.int32, firsts.shape[1:], 1)
-    numbers = jnp.zeros(firsts.shape[1:], jnp.int32)
-    for d in range(devices):
-        numbers = numbers + jnp.where(firsts[d] == lanes, d, 0)
-        numbers = numbers + jnp.where(blocks - 1 - firsts[d] == lanes, d, 0)
-    place_vec[...] = jnp.minimum(numbers, devices - 1)
-    low_blocks(3, {0: [do(side_arrived, 2, 0)], 1: [do(weight_own, last)], 3: [do(far_arrived, 2, 3)]})
+
+    def find_places():
+        lanes = lax.broadcasted_iota(jnp.int32, (1, half), 1)
+        numbers = jnp.zeros((1, half), jnp.int32)
+        for d in range(devices):
+            for i in range(2):
+                numbers = numbers + jnp.where(firsts[d, i : i + 1, :] // half == lanes, d, 0)
+        place_vec[...] = jnp.broadcast_to(jnp.minimum(numbers, devices - 1), place_vec.shape)
+
+    low_blocks([(2, 1), (3, 1)], {0: [do(side_arrived, 2, 0)], 1: [do(weight_own, last), find_places], 2: [do(weight_round, 1)]})
     to_scalars = pltpu.make_async_copy(place_vec, place_ref, place_sem)
     to_scalars.start()
     to_scalars.wait()
 
-    first = first_ref[0]
+    first = order_ref[0] // half
     key_rows = lax.broadcasted_iota(jnp.int32, (span, width), 0)
-    query_cols = lax.broadcasted_iota(jnp.int32, (span, width), 1) % half
+    query_cols = lax.broadcasted_iota(jnp.int32, (span, width), 1) // group
 
     def finish(which, hooks):
         block = blocks - 1 - first if which else first
@@ -533,20 +541,24 @@
             for g in range(group):
                 cols = pl.ds(g * half, half)
                 attended = acc_ref[at, :, cols] / sum_ref[at, :, cols]
+                turn_ref[cols, :] = attended.T
+            for g in range(group):
                 target = pl.ds(pl.multiple_of(h * piece + g * head_size, head_size), head_size)
-                rows_ref[pl.ds(which * half, half), target] = attended.T.astype(jnp.bfloat16)
+                mine = turn_ref[pl.ds(g, half, stride=group), :]
+                rows_ref[pl.ds(which * half, half), target] = mine.astype(jnp.bfloat16)
 
     finish(
         0,
         {
-            0: [do(side_arrived, 2, 1), do(weight_own, 0)],
-            1: [do(weight_round, 1)],
-            4: [do(side_arrived, 2, 2)],
-            5: [do(weight_own, 1)],
-            8: [do(side_arrived, 2, 3), do(weight_own, 2)],
-            10: [do(wfar_arrived, 1, 0)],
-            11: [do(wfar_arrived, 2, 0)],
-            12: [do(weight_round, 2)],
+            0: [do(weight_own, 0)],
+            1: [do(side_arrived, 2, 1)],
+            3: [do(far_arrived, 2, 3)],
+            5: [do(side_arrived, 2, 2), do(weight_own, 1)],
+            8: [do(wfar_arrived, 1, 0), do(weight_own, 2)],
+            9: [do(weight_round, 2)],
+            10: [do(wfar_arrived, 2, 0)],
+            12: [do(side_arrived, 2, 3)],
+            14: [do(wfar_arrived, 1, 1)],
         },
     )
     for hop in range(outers):
@@ -555,32 +567,38 @@
     finish(
         1,
         {
-            1: [do(wside_arrived, 0, last)],
+            0: [do(wside_arrived, 0, last)],
+            1: [do(wfar_arrived, 2, 1)],
             2: [do(wfar_arrived, 3, 0)],
             3: [do(weight_round, last)],
-            4: [do(wfar_arrived, 1, 1)],
             5: [do(wside_arrived, 0, 0)],
-            7: [do(wfar_arrived, 2, 1)],
+            8: [do(wfar_arrived, 1, 2)],
             9: [do(wside_arrived, 0, 1)],
-            11: [do(weight_round, pieces)],
-            12: [do(wfar_arrived, 1, 2)],
-            13: [do(wfar_arrived, 3, 1)],
-            14: [do(wside_arrived, 0, 2)],
-            15: [do(wfar_arrived, 2, 2), do(wside_arrived, 1, 0)],
+            10: [do(weight_round, pieces)],
+            11: [do(wfar_arrived, 2, 2)],
+            12: [do(wfar_arrived, 3, 1)],
+            14: [do(wside_arrived, 0, 2), do(wside_arrived, 1, 0)],
         },
     )
     wside_arrived(2, 0)
     rows_copy(1, kv_heads - 1).start()
 
-    def project(hop, cross):
+    def project(hop, cross, low, high, begin=False, end=False):
         n = hop * 2 + cross
         base = slot_of(hop, cross, 0) - inner
-        for m in range(pieces):
+        for m in range(low, high):
             wpair_copy(hop, cross, m).wait_recv()
-        weight = jnp.concatenate([w_all[base], w_all[base + 1]], axis=1)
+        deep = pl.ds(low * piece, (high - low) * piece)
+        weight = jnp.concatenate([w_all[base, deep, :], w_all[base + 1, deep, :]], axis=1)
         product = lax.dot_general(
-            rows_ref[...], weight, (((1,), (0,)), ((), ())), preferred_element_type=jnp.float32
-        ).astype(jnp.bfloat16)
+            rows_ref[:, deep], weight, (((1,), (0,)), ((), ())), preferred_element_type=jnp.float32
+        )
+        if not begin:
+            product = product + part_ref[n]
+        if not end:
+            part_ref[n] = product
+            return
+        product = product.astype(jnp.bfloat16)
         for i in range(2):
             back_ref[n * 2 + i] = product[tokens:, i * share : (i + 1) * share]
         for i in range(2):
@@ -589,36 +607,21 @@
         for i in range(2):
             back_copy(n * 2 + i, base + i).start()
 
-    wfar_arrived(3, 2)
-    wside_arrived(3, 0)
     for which in range(2):
         for h in range(kv_heads):
             rows_copy(which, h).wait_recv()
+    project(0, 0, 0, pieces, True, True)
+    wside_arrived(3, 0)
     wside_arrived(1, 1)
-    project(0, 0)
+    project(0, 1, 0, pieces, True, True)
+    wfar_arrived(3, 2)
     wfar_arrived(1, last)
     wfar_arrived(2, last)
-    project(0, 1)
+    project(1, 0, 0, last, True)
+    project(2, 0, 0, last, True)
     wside_arrived(2, 1)
     wfar_arrived(1, pieces)
-    wfar_arrived(2, pieces)
-    wside_arrived(3, 1)
-    project(1, 0)
-    wside_arrived(1, 2)
-    project(1, 1)
-    wfar_arrived(3, last)
-    project(2, 0)
-    wside_arrived(2, 2)
-    project(2, 1)
-    wfar_arrived(3, pieces)
-    project(3, 0)
-    wside_arrived(3, 2)
-    project(3, 1)
-
-    for n in range(2 * 2 * outers):
-        back_copy(n, 0).wait_recv()
-    for n in range(2 * 2 * outers):
-        back_copy(n, 0).wait_send()
+
     for which in range(2):
         for h in range(kv_heads):
             rows_copy(which, h).wait_send()
@@ -629,38 +632,75 @@
             side_copy(item, hop).wait_send()
             for cross in range(2):
                 pair_copy(item, hop, cross).wait_send()
-        for n in range(pieces):
-            if hop == 0 or n < last:
-                wside_copy(hop, n).wait_send()
-            for cross in range(2):
-                wpair_copy(hop, cross, n).wait_send()
-        for e in range(pieces + 1):
-            if 0 < hop < 3:
-                wfar_copy(hop, e).wait_send()
+
+    wfar_arrived(2, pieces)
+    project(1, 0, last, pieces, False, True)
+    project(2, 0, last, pieces, False, True)
+    wside_arrived(1, 2)
+    project(1, 1, 0, pieces, True, True)
+    for hop in range(1, 3):
+        for e in range(last):
+            wfar_copy(hop, e).wait_send()
+    for n in range(pieces):
+        wside_copy(0, n).wait_send()
+        for cross in range(2):
+            wpair_copy(0, cross, n).wait_send()
 
     @pl.when(inside)
     def _():
         for item in range(3):
             far_copy(item, 3).wait_send()
             pass_copy(item).wait_send()
-        for e in range(pieces + 1):
+        for e in range(last):
             wfar_copy(3, e).wait_send()
             wpass_copy(e).wait_send()
 
-
-def layer(query_parts, packed, first, out_weight, half):
+    wside_arrived(3, 1)
+    project(3, 0, 0, last, True)
+    wfar_arrived(3, last)
+    wside_arrived(2, 2)
+    project(2, 1, 0, pieces, True, True)
+    project(3, 1, 0, 2, True)
+    wfar_arrived(3, pieces)
+    wside_arrived(3, 2)
+    project(3, 0, last, pieces, False, True)
+    project(3, 1, 2, pieces, False, True)
+
+    for hop in range(1, outers):
+        for n in range(pieces):
+            if n < last:
+                wside_copy(hop, n).wait_send()
+            for cross in range(2):
+                wpair_copy(hop, cross, n).wait_send()
+        for e in range(last, pieces + 1):
+            if hop < 3:
+                wfar_copy(hop, e).wait_send()
+
+    @pl.when(inside)
+    def _():
+        for e in range(last, pieces + 1):
+            wfar_copy(3, e).wait_send()
+            wpass_copy(e).wait_send()
+
+    for n in range(2 * 2 * outers):
+        back_copy(n, 0).wait_send()
+    for n in range(2 * 2 * outers):
+        back_copy(n, 0).wait_recv()
+
+
+def layer(query_states, packed, positions, out_weight, kv_heads):
     devices = lax.axis_size("ctx")
     outers = devices // 4
-    kv_heads, _, width, head_size = query_parts.shape
-    group = width // half
-    tokens = 2 * half
+    tokens, query_heads, head_size = query_states.shape
+    half = tokens // 2
+    group = query_heads // kv_heads
+    width = group * half
     depth, columns = out_weight.shape
     share = columns // 2
     slots = kv_heads + 1
     pieces = kv_heads
-    table = jnp.full((8, 128), first, jnp.int32)
     dma = pltpu.SemaphoreType.DMA
-    flops = 4 * query_parts.size * half * (2 * devices + 1) // 2 + 4 * tokens * depth * columns * devices // 2
+    flops = 4 * query_states.size * half * (2 * devices + 1) // 2 + 4 * tokens * depth * columns * devices // 2
     return pl.pallas_call(
         functools.partial(layer_kernel, (devices, half, kv_heads, group, head_size, share)),
         out_shape=jax.ShapeDtypeStruct((tokens, columns * devices), jnp.bfloat16),
@@ -668,22 +708,26 @@
             pl.BlockSpec(memory_space=pltpu.SMEM),
             pl.BlockSpec(memory_space=pltpu.VMEM),
             pl.BlockSpec(memory_space=pltpu.VMEM),
-            pl.BlockSpec(memory_space=pltpu.VMEM),
+            pl.BlockSpec(memory_space=pl.ANY),
             pl.BlockSpec(memory_space=pl.ANY),
         ],
         out_specs=pl.BlockSpec(memory_space=pltpu.VMEM),
         scratch_shapes=[
             pltpu.VMEM((devices, half, packed.shape[1]), packed.dtype),
             pltpu.VMEM((devices, half, packed.shape[1]), packed.dtype),
-            pltpu.VMEM((devices, 8, 128), jnp.int32),
-            pltpu.VMEM((8, 128), jnp.int32),
-            pltpu.SMEM((8, 128), jnp.int32),
+            pltpu.VMEM((devices, 2, half), jnp.int32),
+            pltpu.VMEM((8, half), jnp.int32),
+            pltpu.SMEM((8, half), jnp.int32),
             pltpu.VMEM((devices, depth, share), out_weight.dtype),
             pltpu.VMEM((slots, head_size, width), jnp.float32),
             pltpu.VMEM((slots, 1, width), jnp.float32),
             pltpu.VMEM((slots, 1, width), jnp.float32),
             pltpu.VMEM((2 * tokens, depth), jnp.bfloat16),
             pltpu.VMEM((devices, tokens, share), jnp.bfloat16),
+            pltpu.VMEM((devices // 2, 2 * tokens, 2 * share), jnp.float32),
+            pltpu.VMEM(query_states.shape, query_states.dtype),
+            pltpu.VMEM((kv_heads, 2, width, head_size), query_states.dtype),
+            pltpu.VMEM((width, head_size), jnp.float32),
             dma((3, outers)),
             dma((3, outers)),
             dma((3, outers)),
@@ -704,13 +748,14 @@
             dma((pieces + 1,)),
             dma,
             dma,
+            dma,
         ],
         compiler_params=pltpu.CompilerParams(
             collective_id=0, has_side_effects=True, vmem_limit_bytes=VMEM
         ),
         cost_estimate=pl.CostEstimate(flops=flops, bytes_accessed=2 * out_weight.size, transcendentals=0),
         name="layer",
-    )(first.reshape(1), table, packed, query_parts, out_weight)
+    )(positions, positions.reshape(2, half), packed, query_states, out_weight)
 
 
 def local(query_states, key_states, value_rows, positions, out_weight):
@@ -723,13 +768,13 @@
     parts = lax.axis_size("groups")
     me_part = lax.axis_index("groups")
     share = out_weight.shape[1] // parts
-    query_parts = query_states.reshape(2, half, kv_heads, group, head_size).transpose(2, 0, 3, 1, 4)
-    query_parts = query_parts.reshape(kv_heads, 2, group * half, head_size)
     if parts == 2 and lax.axis_size("tp") == 1 and devices == 4 * BLOCKS_PER_STEP and share % 128 == 0:
         packed = jnp.concatenate(
             [key_states.reshape(tokens, kv_heads * head_size), value_rows.reshape(tokens, kv_heads * head_size)], axis=1
         )
-        return layer(query_parts, packed, positions[0] // half, out_weight, half)
+        return layer(query_states, packed, positions, out_weight, kv_heads)
+    query_parts = query_states.reshape(2, half, kv_heads, group, head_size).transpose(2, 0, 3, 1, 4)
+    query_parts = query_parts.reshape(kv_heads, 2, group * half, head_size)
     weight_share = lax.dynamic_slice_in_dim(out_weight, me_part * share, share, 1)
     weight = lax.all_gather(weight_share, "ctx", axis=1, tiled=True)
     packed = jnp.concatenate(

time: 159 us -> 148 us (0.931)
  Pallas kernels: 150 us -> 146 us
  local copies, waits for them, and re-layouts: 5.89 us -> 2.43 us
  between operations: 2.64 us -> 0.03 us
    pallas_call x1, Pallas kernels: 150 us -> 146 us  [layer(): pl.pallas_call(functools.partial(layer_kernel, (devices, half, kv_heads,...]
    reshape x1 -> x0, local copies, waits for them, and re-layouts: 2.13 us -> none  [local(): query_states.reshape(2, half, kv_heads, group, head_size)]
where the time goes in v3:
time: 148 us
  Pallas kernels  146 us (99%)
  local copies, waits for them, and re-layouts  2.43 us (2%)
    pallas_call x1, Pallas kernels, layer(): pl.pallas_call(functools.partial(layer_kernel, (devices, half, kv_heads,...  146 us

profile of v3, /device:TPU:0, one launch (start us, length us, event | category | flops | bytes accessed | tf_op | source)
XLA Modules:
  0.0 148.1 jit_solution(13581014561243208811)
XLA Ops:
  0.0 0.0 copy-start
  0.0 1.1 copy_bitcast_fusion
  1.1 0.1 pad_maximum_fusion.kv_ref
  1.2 0.0 copy-done
  1.2 145.6 %layer.1 = bf16[256,4096]{1,0:T(8,128)(2,1)S(1)} custom-call(s32[256]{0:T(256)S(1)} %copy-done, s32[2,128]{1,0:T(2,128)S(1)} %bitcast.7, bf16[256,1024]{1,0:T(8,128)(2,1)S(1)} %pad_maximum_fusion.kv_ref, bf16[256,32,128]{2,1,0:T(8,128)(2,1)} %q_raw.1, bf16[4096,256]{1,0:T(8,128)(2,1)} %w_ref.1), custom_call_target="tpu_custom_call" | custom-call | flops 17448304640 | bytes 2097152 | tf_op jit(solution)/shard_map/layer/pallas_call | solution.py:704
  146.7 1.3 copy.11
Async XLA Ops:
  0.0 1.2 copy-start

commit v4 on v3

--- a/solution.py
+++ b/solution.py
@@ -228,9 +228,8 @@
 def layer_kernel(sizes, order_ref, table_ref, kv_ref, q_raw, w_ref, out_ref, *scratch):
     devices, half, kv_heads, group, head_size, share = sizes
     (kv_low, kv_high, firsts, place_vec, place_ref, w_all, acc_ref, max_ref, sum_ref, rows_ref, back_ref, part_ref, q_in, q_ref, turn_ref, *sems) = scratch
-    (far_send, far_recv, side_send, side_recv, pair_send, pair_recv) = sems[:6]
-    (wfar_send, wfar_recv, wside_send, wside_recv, wpair_send, wpair_recv) = sems[6:12]
-    (rows_send, rows_recv, back_send, back_recv, pass_send, wpass_send, own_sem, place_sem, q_sem) = sems[12:]
+    (far_send, far_recv, side_recv, pair_send, pair_recv, wfar_send, wfar_recv, wside_send, wside_recv) = sems[:9]
+    (wpair_send, wpair_recv, rows_send, rows_recv, back_send, back_recv, own_sem, place_sem, q_sem) = sems[9:]
     outers = devices // 4
     blocks = 2 * devices
     tokens = 2 * half
@@ -291,15 +290,15 @@
         return own_item(item) if hop == 0 and cross == 0 else item_at(item, slot_of(hop, cross, 0))
 
     def far_copy(item, hop):
-        return remote(own_item(item), item_at(item, me), far_send.at[item, hop], far_recv.at[item, hop], "ctx", far[hop])
+        return remote(own_item(item), item_at(item, me), far_send.at[item, hop // 3], far_recv.at[item, hop], "ctx", far[hop])
 
     def pass_copy(item):
         ref = item_at(item, far[2])
-        return remote(ref, ref, pass_send.at[item], far_recv.at[item, 3], "ctx", far[1])
+        return remote(ref, ref, far_send.at[item, 1], far_recv.at[item, 3], "ctx", far[1])
 
     def side_copy(item, hop):
         return remote(
-            source_of(item, hop, 0), item_at(item, far[hop]), side_send.at[item, hop], side_recv.at[item, hop], "ctx", side
+            source_of(item, hop, 0), item_at(item, far[hop]), pair_send.at[item], side_recv.at[item, hop], "ctx", side
         )
 
     def pair_copy(item, hop, cross):
@@ -307,8 +306,8 @@
         return remote(
             source_of(item, hop, cross),
             item_at(item, slot_of(hop, cross, 0)),
-            pair_send.at[item, n],
-            pair_recv.at[item, n],
+            pair_send.at[item],
+            pair_recv.at[n if item == 1 else 2 * outers + item // 2],
             "ctx",
             pair,
         )
@@ -321,34 +320,40 @@
 
     def wfar_copy(hop, e):
         ref = far_part(0, e)
-        return remote(ref, ref, wfar_send.at[hop, e], wfar_recv.at[hop, e], "ctx", far[hop])
+        return remote(ref, ref, wfar_send.at[hop], wfar_recv.at[hop, e], "ctx", far[hop])
 
     def wpass_copy(e):
         ref = far_part(2, e)
-        return remote(ref, ref, wpass_send.at[e], wfar_recv.at[3, e], "ctx", far[1])
+        return remote(ref, ref, wfar_send.at[0], wfar_recv.at[3, e], "ctx", far[1])
 
     def wside_copy(hop, n):
         ref = w_at(far[hop], n)
-        return remote(ref, ref, wside_send.at[hop, n], wside_recv.at[hop, n], "ctx", side)
+        return remote(ref, ref, wside_send.at[min(hop, 1)], wside_recv.at[hop, n], "ctx", side)
 
     def wpair_copy(hop, cross, n):
         ref = w_at(slot_of(hop, cross, 0), n)
-        return remote(ref, ref, wpair_send.at[hop * 2 + cross, n], wpair_recv.at[hop * 2 + cross, n], "ctx", pair)
+        return remote(ref, ref, wpair_send.at[hop], wpair_recv.at[hop * 2 + cross, n], "ctx", pair)
 
     def rows_copy(which, h):
         cols = pl.ds(pl.multiple_of(h * piece, piece), piece)
         return remote(
             rows_ref.at[pl.ds(which * half, half), cols],
             rows_ref.at[pl.ds(tokens + which * half, half), cols],
-            rows_send.at[which, h],
-            rows_recv.at[which, h],
+            rows_send,
+            rows_recv,
             "groups",
             guest,
         )
 
     def back_copy(n, slot):
         cols = pl.ds(pl.multiple_of((slot * 2 + part) * share, share), share)
-        return remote(back_ref.at[n], out_ref.at[:, cols], back_send.at[n], back_recv.at[n], "groups", guest)
+        return remote(back_ref.at[n], out_ref.at[:, cols], back_send, back_recv, "groups", guest)
+
+    def all_sent(ref, sem):
+        remote(ref, ref, sem, sem, "ctx", pair).wait_send()
+
+    def all_landed(ref, sem):
+        remote(ref, ref, sem, sem, "ctx", pair).wait_recv()
 
     def far_start(copy, hop):
         if hop == 3:
@@ -375,10 +380,6 @@
     def side_arrived(item, hop):
         side_copy(item, hop).wait_recv()
         pair_copy(item, hop, 1).start()
-
-    def pair_arrived(item, hop):
-        for cross in range(2):
-            pair_copy(item, hop, cross).wait_recv()
 
     def wfar_arrived(hop, e):
         wfar_copy(hop, e).wait_recv()
@@ -460,8 +461,7 @@
     def low_blocks(parts, hooks):
         places = [slot_of(hop, cross, swap) for hop, cross in parts for swap in range(2)]
         for hop, cross in parts:
-            for item in range(2):
-                pair_copy(item, hop, cross).wait_recv()
+            pair_copy(1, hop, cross).wait_recv()
 
         @pl.loop(0, kv_heads)
         def _(h):
@@ -488,10 +488,11 @@
         return functools.partial(action, *args)
 
     low_side(0)
-    low_blocks([(0, 0), (0, 1)], {3: [do(low_far, 1)]})
+    side_copy(2, 0).start()
+    low_blocks([(0, 0), (0, 1)], {2: [do(low_far, 1)]})
     low_far(2)
     own_start(2)
-    low_blocks([(1, 0), (2, 0)], {2: [side_copy(2, 0).start]})
+    low_blocks([(1, 0), (2, 0)], {})
     low_side(1)
     low_far(3)
     low_blocks([(1, 1), (3, 0)], {1: [do(low_side, 2)], 3: [do(far_arrived, 2, 1)]})
@@ -500,6 +501,7 @@
     low_side(3)
 
     def find_places():
+        all_landed(firsts.at[pl.ds(0, 2 * outers)], pair_recv.at[2 * outers])
         lanes = lax.broadcasted_iota(jnp.int32, (1, half), 1)
         numbers = jnp.zeros((1, half), jnp.int32)
         for d in range(devices):
@@ -561,8 +563,7 @@
             14: [do(wfar_arrived, 1, 1)],
         },
     )
-    for hop in range(outers):
-        pair_arrived(2, hop)
+    all_landed(kv_high.at[pl.ds(0, 2 * outers)], pair_recv.at[2 * outers + 1])
     rows_copy(0, kv_heads - 1).start()
     finish(
         1,
@@ -607,85 +608,53 @@
         for i in range(2):
             back_copy(n * 2 + i, base + i).start()
 
-    for which in range(2):
-        for h in range(kv_heads):
-            rows_copy(which, h).wait_recv()
+    all_landed(rows_ref.at[pl.ds(tokens, tokens), :], rows_recv)
     project(0, 0, 0, pieces, True, True)
     wside_arrived(3, 0)
     wside_arrived(1, 1)
+    wfar_arrived(3, 2)
     project(0, 1, 0, pieces, True, True)
-    wfar_arrived(3, 2)
     wfar_arrived(1, last)
     wfar_arrived(2, last)
     project(1, 0, 0, last, True)
-    project(2, 0, 0, last, True)
     wside_arrived(2, 1)
     wfar_arrived(1, pieces)
-
-    for which in range(2):
-        for h in range(kv_heads):
-            rows_copy(which, h).wait_send()
-    for hop in range(outers):
-        for item in range(3):
-            if 0 < hop < 3:
-                far_copy(item, hop).wait_send()
-            side_copy(item, hop).wait_send()
-            for cross in range(2):
-                pair_copy(item, hop, cross).wait_send()
-
+    project(2, 0, 0, last, True)
+    all_sent(rows_ref.at[pl.ds(0, tokens), :], rows_send)
+    for item, ref in enumerate((firsts, kv_low, kv_high)):
+        all_sent(ref.at[pl.ds(0, 2)], far_send.at[item, 0])
+        all_sent(ref.at[pl.ds(0, 3 * outers)], pair_send.at[item])
     wfar_arrived(2, pieces)
     project(1, 0, last, pieces, False, True)
     project(2, 0, last, pieces, False, True)
     wside_arrived(1, 2)
     project(1, 1, 0, pieces, True, True)
-    for hop in range(1, 3):
-        for e in range(last):
-            wfar_copy(hop, e).wait_send()
-    for n in range(pieces):
-        wside_copy(0, n).wait_send()
-        for cross in range(2):
-            wpair_copy(0, cross, n).wait_send()
+    project(3, 0, 0, last, True)
+    project(2, 1, 0, 2, True)
+    wside_arrived(3, 1)
+    wfar_arrived(3, last)
+    project(3, 0, last, pieces, False, True)
+    wside_arrived(2, 2)
+    wfar_arrived(3, pieces)
+    wside_arrived(3, 2)
+    project(2, 1, 2, pieces, False, True)
+    project(3, 1, 0, pieces, True, True)
 
     @pl.when(inside)
     def _():
-        for item in range(3):
-            far_copy(item, 3).wait_send()
-            pass_copy(item).wait_send()
-        for e in range(last):
-            wfar_copy(3, e).wait_send()
-            wpass_copy(e).wait_send()
-
-    wside_arrived(3, 1)
-    project(3, 0, 0, last, True)
-    wfar_arrived(3, last)
-    wside_arrived(2, 2)
-    project(2, 1, 0, pieces, True, True)
-    project(3, 1, 0, 2, True)
-    wfar_arrived(3, pieces)
-    wside_arrived(3, 2)
-    project(3, 0, last, pieces, False, True)
-    project(3, 1, 2, pieces, False, True)
-
-    for hop in range(1, outers):
-        for n in range(pieces):
-            if n < last:
-                wside_copy(hop, n).wait_send()
-            for cross in range(2):
-                wpair_copy(hop, cross, n).wait_send()
-        for e in range(last, pieces + 1):
-            if hop < 3:
-                wfar_copy(hop, e).wait_send()
-
-    @pl.when(inside)
-    def _():
-        for e in range(last, pieces + 1):
-            wfar_copy(3, e).wait_send()
-            wpass_copy(e).wait_send()
-
-    for n in range(2 * 2 * outers):
-        back_copy(n, 0).wait_send()
-    for n in range(2 * 2 * outers):
-        back_copy(n, 0).wait_recv()
+        for item, ref in enumerate((firsts, kv_low, kv_high)):
+            all_sent(ref.at[pl.ds(0, 2)], far_send.at[item, 1])
+        for i in (0, 3):
+            all_sent(w_all.at[pl.ds(0, pieces + 1), pl.ds(0, piece), :], wfar_send.at[i])
+
+    for hop in range(1, 3):
+        all_sent(w_all.at[pl.ds(0, pieces + 1), pl.ds(0, piece), :], wfar_send.at[hop])
+    all_sent(w_all.at[0], wside_send.at[0])
+    all_sent(w_all.at[pl.ds(0, outers - 1), pl.ds(0, last * piece), :], wside_send.at[1])
+    for hop in range(outers):
+        all_sent(w_all.at[pl.ds(0, 2)], wpair_send.at[hop])
+    all_sent(back_ref, back_send)
+    all_landed(back_ref, back_recv)
 
 
 def layer(query_states, packed, positions, out_weight, kv_heads):
@@ -728,24 +697,21 @@
             pltpu.VMEM(query_states.shape, query_states.dtype),
             pltpu.VMEM((kv_heads, 2, width, head_size), query_states.dtype),
             pltpu.VMEM((width, head_size), jnp.float32),
+            dma((3, 2)),
             dma((3, outers)),
             dma((3, outers)),
-            dma((3, outers)),
-            dma((3, outers)),
-            dma((3, 2 * outers)),
-            dma((3, 2 * outers)),
+            dma((3,)),
+            dma((2 * outers + 2,)),
+            dma((outers,)),
             dma((outers, pieces + 1)),
-            dma((outers, pieces + 1)),
+            dma((2,)),
             dma((outers, pieces)),
-            dma((outers, pieces)),
+            dma((outers,)),
             dma((2 * outers, pieces)),
-            dma((2 * outers, pieces)),
-            dma((2, kv_heads)),
-            dma((2, kv_heads)),
-            dma((devices,)),
-            dma((devices,)),
-            dma((3,)),
-            dma((pieces + 1,)),
+            dma,
+            dma,
+            dma,
+            dma,
             dma,
             dma,
             dma,

time: 148 us -> 144 us (0.973)
  Pallas kernels: 146 us -> 141 us
    pallas_call x1, Pallas kernels: 146 us -> 141 us  [layer(): pl.pallas_call(functools.partial(layer_kernel, (devices, half, kv_heads,...]
where the time goes in v4:
time: 144 us
  Pallas kernels  141 us (98%)
  local copies, waits for them, and re-layouts  2.43 us (2%)
    pallas_call x1, Pallas kernels, layer(): pl.pallas_call(functools.partial(layer_kernel, (devices, half, kv_heads,...  141 us

profile of v4, /device:TPU:0, one launch (start us, length us, event | category | flops | bytes accessed | tf_op | source)
XLA Modules:
  0.0 143.7 jit_solution(17599250772184833675)
XLA Ops:
  0.0 0.0 copy-start
  0.0 1.1 copy_bitcast_fusion
  1.1 0.1 pad_maximum_fusion.kv_ref
  1.2 0.0 copy-done
  1.2 141.2 %layer.1 = bf16[256,4096]{1,0:T(8,128)(2,1)S(1)} custom-call(s32[256]{0:T(256)S(1)} %copy-done, s32[2,128]{1,0:T(2,128)S(1)} %bitcast.7, bf16[256,1024]{1,0:T(8,128)(2,1)S(1)} %pad_maximum_fusion.kv_ref, bf16[256,32,128]{2,1,0:T(8,128)(2,1)} %q_raw.1, bf16[4096,256]{1,0:T(8,128)(2,1)} %w_ref.1), custom_call_target="tpu_custom_call" | custom-call | flops 17448304640 | bytes 2097152 | tf_op jit(solution)/shard_map/layer/pallas_call | solution.py:673
  142.4 1.3 copy.11
Async XLA Ops:
  0.0 1.2 copy-start

commit v5 on v4

--- a/solution.py
+++ b/solution.py
@@ -549,6 +549,11 @@
                 mine = turn_ref[pl.ds(g, half, stride=group), :]
                 rows_ref[pl.ds(which * half, half), target] = mine.astype(jnp.bfloat16)
 
+    def far_last(where):
+        @pl.when(where)
+        def _():
+            wfar_arrived(2, 2)
+
     finish(
         0,
         {
@@ -559,8 +564,8 @@
             8: [do(wfar_arrived, 1, 0), do(weight_own, 2)],
             9: [do(weight_round, 2)],
             10: [do(wfar_arrived, 2, 0)],
-            12: [do(side_arrived, 2, 3)],
-            14: [do(wfar_arrived, 1, 1)],
+            13: [do(wfar_arrived, 1, 1)],
+            15: [do(side_arrived, 2, 3)],
         },
     )
     all_landed(kv_high.at[pl.ds(0, 2 * outers)], pair_recv.at[2 * outers + 1])
@@ -576,13 +581,15 @@
             8: [do(wfar_arrived, 1, 2)],
             9: [do(wside_arrived, 0, 1)],
             10: [do(weight_round, pieces)],
-            11: [do(wfar_arrived, 2, 2)],
+            11: [do(far_last, inside)],
             12: [do(wfar_arrived, 3, 1)],
-            14: [do(wside_arrived, 0, 2), do(wside_arrived, 1, 0)],
+            13: [do(wside_arrived, 0, 2)],
+            14: [do(wside_arrived, 1, 0)],
         },
     )
     wside_arrived(2, 0)
     rows_copy(1, kv_heads - 1).start()
+    far_last(jnp.logical_not(inside))
 
     def project(hop, cross, low, high, begin=False, end=False):
         n = hop * 2 + cross
@@ -630,15 +637,16 @@
     wside_arrived(1, 2)
     project(1, 1, 0, pieces, True, True)
     project(3, 0, 0, last, True)
-    project(2, 1, 0, 2, True)
     wside_arrived(3, 1)
     wfar_arrived(3, last)
+    project(2, 1, 0, 2, True)
     project(3, 0, last, pieces, False, True)
     wside_arrived(2, 2)
     wfar_arrived(3, pieces)
+    project(3, 1, 0, 1, True)
     wside_arrived(3, 2)
     project(2, 1, 2, pieces, False, True)
-    project(3, 1, 0, pieces, True, True)
+    project(3, 1, 1, pieces, False, True)
 
     @pl.when(inside)
     def _():

time: 144 us -> 144 us (level)
  no operation moved by 1% of the time
where the time goes in v5:
time: 144 us
  Pallas kernels  141 us (98%)
  local copies, waits for them, and re-layouts  2.43 us (2%)
    pallas_call x1, Pallas kernels, layer(): pl.pallas_call(functools.partial(layer_kernel, (devices, half, kv_heads,...  141 us

profile of v5, /device:TPU:0, one launch (start us, length us, event | category | flops | bytes accessed | tf_op | source)
XLA Modules:
  0.0 143.7 jit_solution(14249697596154414977)
XLA Ops:
  0.0 0.0 copy-start
  0.0 1.1 copy_bitcast_fusion
  1.1 0.1 pad_maximum_fusion.kv_ref
  1.2 0.0 copy-done
  1.2 141.2 %layer.1 = bf16[256,4096]{1,0:T(8,128)(2,1)S(1)} custom-call(s32[256]{0:T(256)S(1)} %copy-done, s32[2,128]{1,0:T(2,128)S(1)} %bitcast.7, bf16[256,1024]{1,0:T(8,128)(2,1)S(1)} %pad_maximum_fusion.kv_ref, bf16[256,32,128]{2,1,0:T(8,128)(2,1)} %q_raw.1, bf16[4096,256]{1,0:T(8,128)(2,1)} %w_ref.1), custom_call_target="tpu_custom_call" | custom-call | flops 17448304640 | bytes 2097152 | tf_op jit(solution)/shard_map/layer/pallas_call | solution.py:681
  142.3 1.3 copy.11
Async XLA Ops:
  0.0 1.2 copy-start
